TPU v7x, 128 devices: a whole 4x4x4 slice. The times are simulated.
128 devices in a mesh: space: 8 (over z_lo, x), mode: 16 (over z_hi, y, core).
Axes of the slice: x: 4, y: 4, z: 4 (z_hi: 2, z_lo: 2; z = z_hi * 2 + z_lo), core: 2. Of those that a mesh axis runs over, the one named last changes fastest.
Arguments:
- excess_phonon_enthalpy: bfloat16 [768, 64, 128, 128], P('mode', 'space'), may hold values from -0.21972656 to 0.21972656
- thermal_offset: float32 [128, 128, 64], P('space', 'mode'), may hold values from -6 to 6
- state_specific_warmth_scaled: float32 [768], P('mode'), may hold values from 0.5 to 2
- scattering_lifetimes: float32 [768], P('mode'), may hold values from 0.5 to 50
- state_polarization_label: int32 [768], P('mode'), may hold values from 0 to 5
- state_orientation_label: int32 [768], P('mode'), may hold values from 0 to 15
- polarization_propagation_rate: float32 [6], replicated, may hold values from 0.3 to 1
- thermal_conductance_bulk: float32 [128, 128, 64], P('space', 'mode'), may hold values from 0.25 to 1
- substance_label: int32 [128, 128, 64], P('space', 'mode'), may hold values 0 or 1
Outputs:
- final_temperature: float32 [128, 128, 64], P('space', 'mode')
- heat_flux: float32 [3, 128, 128, 64], P(None, 'space', 'mode')
Inputs may be any that keep to these rules, and one draw needn't show every extreme that they name: `substance_label`: 1 marks a pore cell.
All inputs are finite; a program needn't handle non-finite values. No bound on the sum of `substance_label` on one device may be relied on, other than what follows from the above.
Results may differ from a plain program's by a relative error of at most 0.0028.
Values may be sent and summed in bfloat16 or wider, within the bound.
No kernel may reach another device: no remote copies, remote signals or barrier semaphores. Data moves between devices by JAX's collectives and lax.ppermute only.
A program may use at most 128 MiB of HBM per device.

v0:
```python
import math

import jax
import jax.numpy as jnp
from jax import lax
from jax.sharding import PartitionSpec as P

M = 768
SWEEPS = 4
OUTER = 2


time_step = 0.25
pore_factor = 0.1
kappa_top = 1.0


def padded_2(cells, sides, width):
    for axis, dim in sides:
        count = lax.axis_size(axis)
        ends = count - 1
        head = lax.slice_in_dim(cells, 0, width, axis=dim)
        tail = lax.slice_in_dim(cells, cells.shape[dim] - width, cells.shape[dim], axis=dim)
        cells = jnp.concatenate(
            [
                lax.ppermute(tail, axis, [(i, (i + 1) % count) for i in range(ends)]),
                cells,
                lax.ppermute(head, axis, [((i + 1) % count, i) for i in range(ends)]),
            ],
            axis=dim,
        )
    return cells


def sent_to_all(shard, axis):
    copies = jnp.broadcast_to(shard, (lax.axis_size(axis), *shard.shape))
    return lax.all_to_all(copies, axis, split_axis=0, concat_axis=0, tiled=True)


def over_copies(shard, axis):
    everything = sent_to_all(shard, axis)
    return jnp.sum(everything, axis=0)


def in_blocks(shard, dim, length):
    before, after = (shard.shape[:dim], shard.shape[dim + 1 :])
    return jnp.moveaxis(shard.reshape(*before, length, -1, *after), dim, 0)


def sum_at_owner(shard, axis, dim):
    length = lax.axis_size(axis)
    pieces = lax.all_to_all(in_blocks(shard, dim, length), axis, 0, 0, tiled=True)
    return jnp.sum(pieces, axis=0)


def mode_table(
    state_polarization_label,
    state_orientation_label,
    state_specific_warmth_scaled,
    scattering_lifetimes,
    polarization_propagation_rate,
):
    branches = jnp.arange(polarization_propagation_rate.shape[0], dtype=jnp.int32)
    onehot = (state_polarization_label[:, None] == branches[None, :]).astype(jnp.float32)
    speed = jnp.sum(onehot * polarization_propagation_rate[None, :], axis=1)
    polar = state_orientation_label // 4
    azimuth = state_orientation_label % 4
    cosine = (2 * polar + 1).astype(jnp.float32) * 0.25 - 1.0
    sine = jnp.sqrt(1.0 - cosine * cosine)
    angle = (azimuth.astype(jnp.float32) + 0.5) * (math.pi / 2.0)
    velocity = (speed * sine * jnp.cos(angle), speed * sine * jnp.sin(angle), speed * cosine)
    rates = 1.0 / scattering_lifetimes
    capacity = state_specific_warmth_scaled / float(M)
    return (velocity, rates, capacity)


def upwind(padded, temp_slab, along_x, along_y, along_z, rates, capacity):

    def widen(values):
        return values[:, None, None, None]

    current = padded[:, 1:-1]
    z_before = padded[:, :-2]
    z_after = padded[:, 2:]
    x_padded = jnp.pad(current, ((0, 0), (0, 0), (1, 1), (0, 0)))
    y_padded = jnp.pad(current, ((0, 0), (0, 0), (0, 0), (1, 1)))

    def advect(speed, before, after):
        flow = widen(speed)
        return jnp.maximum(flow, 0.0) * (current - before) + jnp.minimum(flow, 0.0) * (
            after - current
        )

    total_advect = advect(along_x, x_padded[:, :, :-2], x_padded[:, :, 2:])
    total_advect = total_advect + advect(along_y, y_padded[:, :, :, :-2], y_padded[:, :, :, 2:])
    total_advect = total_advect + advect(along_z, z_before, z_after)
    updated = (
        current
        - time_step * total_advect
        + time_step * widen(rates) * (widen(capacity) * temp_slab[None] - current)
    )
    weights = jnp.stack([rates, along_x, along_y, along_z])
    moments = jnp.einsum("km,mzxy->kzxy", weights, updated, precision=lax.Precision.HIGHEST)
    return (updated, moments)


def harmonic(first, second):
    summed = first + second
    positive = summed > 0.0
    return jnp.where(positive, 2.0 * first * second / jnp.where(positive, summed, 1.0), 0.0)


def face_table(kappa_ext):
    center = kappa_ext[1:-1, 1:-1]
    z_padded = jnp.pad(center, ((0, 0), (0, 0), (1, 1)))
    return (
        harmonic(center, kappa_ext[2:, 1:-1]),
        harmonic(kappa_ext[:-2, 1:-1], center),
        harmonic(center, kappa_ext[1:-1, 2:]),
        harmonic(kappa_ext[1:-1, :-2], center),
        harmonic(center, z_padded[:, :, 2:]),
        harmonic(z_padded[:, :, :-2], center),
    )


def crop(values, matrix_height, matrix_breadth):
    top = (values.shape[0] - matrix_height) // 2
    left = (values.shape[1] - matrix_breadth) // 2
    return values[top : top + matrix_height, left : left + matrix_breadth]


def apply_operator(padded, faces, total):
    matrix_height = padded.shape[0] - 2
    matrix_breadth = padded.shape[1] - 2
    cut = [crop(face, matrix_height, matrix_breadth) for face in faces]
    center = padded[1:-1, 1:-1]
    z_padded = jnp.pad(center, ((0, 0), (0, 0), (1, 1)))
    spread = cut[0] * (padded[2:, 1:-1] - center) + cut[1] * (padded[:-2, 1:-1] - center)
    spread = spread + cut[2] * (padded[1:-1, 2:] - center) + cut[3] * (padded[1:-1, :-2] - center)
    spread = (
        spread + cut[4] * (z_padded[:, :, 2:] - center) + cut[5] * (z_padded[:, :, :-2] - center)
    )
    return total * center - spread


def divergence(fluxes):
    z_flux = jnp.pad(fluxes[2][1:-1, 1:-1], ((0, 0), (0, 0), (1, 1)))
    summed = (
        fluxes[0][2:, 1:-1] - fluxes[0][:-2, 1:-1] + (fluxes[1][1:-1, 2:] - fluxes[1][1:-1, :-2])
    )
    summed = summed + (z_flux[:, :, 2:] - z_flux[:, :, :-2])
    return summed * 0.5


def chebyshev(rhs, faces, total, extend, matrix_height, matrix_breadth):
    theta = total + 6.0 * kappa_top
    spread = 6.0 * kappa_top
    sigma = theta / spread
    rho = 1.0 / sigma
    residual = rhs
    direction = rhs / theta
    correction = jnp.zeros((matrix_height, matrix_breadth, rhs.shape[2]), jnp.float32)
    for sweep in range(SWEEPS):
        correction = correction + crop(direction, matrix_height, matrix_breadth)
        if sweep < SWEEPS - 1:
            image = apply_operator(extend(direction), faces, total)
            residual = crop(residual, image.shape[0], image.shape[1]) - image
            rho_next = 1.0 / (2.0 * sigma - rho)
            direction = (
                rho_next * rho * crop(direction, image.shape[0], image.shape[1])
                + 2.0 * rho_next / spread * residual
            )
            rho = rho_next
    return correction


def unchanged(direction):
    return direction


def to_slab(block):
    upright = jnp.transpose(block, (2, 0, 1))
    moved = lax.all_to_all(upright, "space", split_axis=0, concat_axis=1, tiled=True)
    return lax.all_gather(moved, "mode", axis=2, tiled=True)


def kinetic(state, temp_slab, velocity, rates, capacity):
    padded = padded_2(state, (("space", 1),), 1)
    local = padded.shape[0]
    group = math.gcd(local, 8)
    count = local // group
    shaped = padded.reshape((count, group) + padded.shape[1:])
    params = (
        velocity[0].reshape(count, group),
        velocity[1].reshape(count, group),
        velocity[2].reshape(count, group),
        rates.reshape(count, group),
        capacity.reshape(count, group),
    )

    def step(carry, inputs):
        block, along_x, along_y, along_z, rate_part, cap_part = inputs
        updated, moments = upwind(
            block.astype(jnp.float32), temp_slab, along_x, along_y, along_z, rate_part, cap_part
        )
        return (carry + moments, updated.astype(jnp.bfloat16))

    start = jnp.zeros((4,) + state.shape[1:], jnp.float32)
    moments, news = lax.scan(step, start, (shaped,) + params)
    return (news.reshape(state.shape), moments)


def per_device(
    excess_phonon_enthalpy,
    thermal_offset,
    state_specific_warmth_scaled,
    scattering_lifetimes,
    state_polarization_label,
    state_orientation_label,
    polarization_propagation_rate,
    thermal_conductance_bulk,
    substance_label,
):
    velocity, rates, capacity = mode_table(
        state_polarization_label,
        state_orientation_label,
        state_specific_warmth_scaled,
        scattering_lifetimes,
        polarization_propagation_rate,
    )
    total = over_copies(jnp.sum(capacity * rates), "mode")
    kappa = thermal_conductance_bulk * jnp.where(substance_label == 1, pore_factor, 1.0)
    matrix_height = thermal_offset.shape[0]
    matrix_breadth = thermal_offset.shape[1]
    kappa_ext = padded_2(kappa.astype(jnp.bfloat16), (("space", 0), ("mode", 1)), SWEEPS).astype(
        kappa.dtype
    )
    faces = face_table(kappa_ext)
    spatial_entries = thermal_offset
    state = excess_phonon_enthalpy
    fluxes = None
    for outer in range(OUTER):
        temp_slab = to_slab(spatial_entries)
        state, moments = kinetic(state, temp_slab, velocity, rates, capacity)
        reduced = sum_at_owner(moments, "mode", 3)
        summed = lax.all_to_all(reduced, "space", split_axis=2, concat_axis=1, tiled=True)
        blocks = jnp.transpose(summed, (0, 2, 3, 1))
        fluxes = blocks[1:]
        flux_ext = padded_2(
            fluxes.astype(jnp.bfloat16), (("space", 1), ("mode", 2)), SWEEPS
        ).astype(fluxes.dtype)
        rhs = -divergence(flux_ext)
        correction = chebyshev(rhs, faces, total, unchanged, matrix_height, matrix_breadth)
        spatial_entries = blocks[0] / total + correction
    return (spatial_entries, fluxes)


def solution(mesh):
    placed = (
        P("mode", "space", None, None),
        P("space", "mode", None),
        P("mode"),
        P("mode"),
        P("mode"),
        P("mode"),
        P(),
        P("space", "mode", None),
        P("space", "mode", None),
    )
    return jax.shard_map(
        per_device,
        mesh=mesh,
        in_specs=placed,
        out_specs=(P("space", "mode", None), P(None, "space", "mode", None)),
        check_vma=False,
    )
```

profile of v0, /device:TPU:70, one launch (start us, length us, event | category | flops | bytes accessed | tf_op | source)
XLA Modules:
  0.0 614.7 jit_solution(17676936092251280161)
XLA Ops:
  0.7 4.0 fusion.165
  11.5 6.8 %all-to-all-start = ((f32[8,1,1024]{2,1,0:T(1,128)}), f32[8,1,1024]{2,1,0:T(1,128)S(1)}, u32[]{:S(2)}, u32[]{:S(2)}) async-start(f32[8,1,1024]{2,1,0:T(1,128)} %reshape.250), calls=%async_computation | async-start | bytes 65536 | tf_op jit(solution)/shard_map/all_to_all | solution.py:183
  19.5 29.1 %all-to-all-done = f32[8,1,1024]{2,1,0:T(1,128)S(1)} async-done(((f32[8,1,1024]{2,1,0:T(1,128)}), f32[8,1,1024]{2,1,0:T(1,128)S(1)}, u32[]{:S(2)}, u32[]{:S(2)}) %all-to-all-start) | async-done | bytes 32800 | tf_op jit(solution)/shard_map/all_to_all | solution.py:183
  49.9 7.5 %all-to-all-start.3 = ((f32[16,1,1]{2,1,0:T(1,128)}), f32[16,1,1]{2,1,0:T(1,128)S(1)}, u32[]{:S(2)}, u32[]{:S(2)}) async-start(f32[16,1,1]{2,1,0:T(1,128)} %broadcast_in_dim.52), calls=%async_computation.3 | async-start | bytes 16384 | tf_op jit(solution)/shard_map/all_to_all | solution.py:37
  59.0 23.0 %all_gather.6 = f32[8,128,128]{1,2,0:T(8,128)S(1)} all-gather(f32[8,128,8]{1,2,0:T(8,128)S(1)} %all_to_all.65), channel_id=1, replica_groups=mesh['space'=8,'mode'=16] {'mode'}, dimensions={2}, use_global_device_ids=true | all-gather | bytes 557056 | tf_op jit(solution)/shard_map/all_gather | solution.py:184
  82.3 13.3 %pad_maximum_fusion = bf16[48,10,128,128]{3,2,1,0:T(8,128)(2,1)} fusion(bf16[48,1,128,128]{3,2,1,0:T(8,128)(2,1)} %collective-permute-done.1, bf16[48,8,128,128]{3,2,1,0:T(8,128)(2,1)} %param.13, bf16[48,1,128,128]{3,2,1,0:T(8,128)(2,1)} %collective-permute-done), kind=kLoop, calls=%fused_computation.96 | loop fusion | flops 15728640 | bytes 31457280 | tf_op jit(solution)/shard_map/concatenate | solution.py:24
  95.6 99.1 %while.28 = (s32[]{:T(128)}, f32[4,8,128,128]{3,0,2,1:T(4,128)S(1)}, bf16[6,8,8,128,128]{4,1,3,2,0:T(8,128)(2,1)}, f32[6,8]{1,0:T(8,128)S(1)}, f32[6,8]{1,0:T(8,...) while((s32[]{:T(128)}, ...), condition=%wide.region_2.3_spmd.clone, body=%wide.region_1.2_spmd.clone.sunk | while | flops 77856920 | bytes 49284748 | solution.py:209
  99.8 5.3 bitcast_dynamic-update-slice_fusion.2
  105.1 7.0 %select_add_fusion.4 = f32[4,8,128,128]{3,0,2,1:T(4,128)S(1)} fusion(f32[4,8,128,128]{3,0,2,1:T(4,128)S(1)} %get-tuple-element.704, f32[8,8,128,128]{3,0,2,1:T(8,128)} %get-tuple-element.671, pred[]{:T(512)S(6)} %compare.22, f32[1,8]{1,0:T(1,128)S(1)} %get-tuple-element.665, f32[1,8]{1,0:T(1,128)S(1)} %get-tuple-element.667, ...), kind=kOutput, calls=%fused_computation.20.clone.1 | convolution fusion | flops 51380320 | bytes 8388737 | tf_op jit(solution)/shard_map/while/body/eval_jaxpr/km,mzxy->kzxy/dot_general | solution.py:103
  116.3 5.3 bitcast_dynamic-update-slice_fusion.2
  121.6 7.0 %select_add_fusion.4 = f32[4,8,128,128]{3,0,2,1:T(4,128)S(1)} fusion(f32[4,8,128,128]{3,0,2,1:T(4,128)S(1)} %get-tuple-element.704, f32[8,8,128,128]{3,0,2,1:T(8,128)} %get-tuple-element.671, pred[]{:T(512)S(6)} %compare.22, f32[1,8]{1,0:T(1,128)S(1)} %get-tuple-element.665, f32[1,8]{1,0:T(1,128)S(1)} %get-tuple-element.667, ...), kind=kOutput, calls=%fused_computation.20.clone.1 | convolution fusion | flops 51380320 | bytes 8388737 | tf_op jit(solution)/shard_map/while/body/eval_jaxpr/km,mzxy->kzxy/dot_general | solution.py:103
  132.8 5.4 bitcast_dynamic-update-slice_fusion.2
  138.2 7.0 %select_add_fusion.4 = f32[4,8,128,128]{3,0,2,1:T(4,128)S(1)} fusion(f32[4,8,128,128]{3,0,2,1:T(4,128)S(1)} %get-tuple-element.704, f32[8,8,128,128]{3,0,2,1:T(8,128)} %get-tuple-element.671, pred[]{:T(512)S(6)} %compare.22, f32[1,8]{1,0:T(1,128)S(1)} %get-tuple-element.665, f32[1,8]{1,0:T(1,128)S(1)} %get-tuple-element.667, ...), kind=kOutput, calls=%fused_computation.20.clone.1 | convolution fusion | flops 51380320 | bytes 8388737 | tf_op jit(solution)/shard_map/while/body/eval_jaxpr/km,mzxy->kzxy/dot_general | solution.py:103
  149.4 5.3 bitcast_dynamic-update-slice_fusion.2
  154.7 7.0 %select_add_fusion.4 = f32[4,8,128,128]{3,0,2,1:T(4,128)S(1)} fusion(f32[4,8,128,128]{3,0,2,1:T(4,128)S(1)} %get-tuple-element.704, f32[8,8,128,128]{3,0,2,1:T(8,128)} %get-tuple-element.671, pred[]{:T(512)S(6)} %compare.22, f32[1,8]{1,0:T(1,128)S(1)} %get-tuple-element.665, f32[1,8]{1,0:T(1,128)S(1)} %get-tuple-element.667, ...), kind=kOutput, calls=%fused_computation.20.clone.1 | convolution fusion | flops 51380320 | bytes 8388737 | tf_op jit(solution)/shard_map/while/body/eval_jaxpr/km,mzxy->kzxy/dot_general | solution.py:103
  165.9 5.3 bitcast_dynamic-update-slice_fusion.2
  171.2 7.0 %select_add_fusion.4 = f32[4,8,128,128]{3,0,2,1:T(4,128)S(1)} fusion(f32[4,8,128,128]{3,0,2,1:T(4,128)S(1)} %get-tuple-element.704, f32[8,8,128,128]{3,0,2,1:T(8,128)} %get-tuple-element.671, pred[]{:T(512)S(6)} %compare.22, f32[1,8]{1,0:T(1,128)S(1)} %get-tuple-element.665, f32[1,8]{1,0:T(1,128)S(1)} %get-tuple-element.667, ...), kind=kOutput, calls=%fused_computation.20.clone.1 | convolution fusion | flops 51380320 | bytes 8388737 | tf_op jit(solution)/shard_map/while/body/eval_jaxpr/km,mzxy->kzxy/dot_general | solution.py:103
  182.4 5.3 bitcast_dynamic-update-slice_fusion.2
  187.7 7.0 %select_add_fusion.4 = f32[4,8,128,128]{3,0,2,1:T(4,128)S(1)} fusion(f32[4,8,128,128]{3,0,2,1:T(4,128)S(1)} %get-tuple-element.704, f32[8,8,128,128]{3,0,2,1:T(8,128)} %get-tuple-element.671, pred[]{:T(512)S(6)} %compare.22, f32[1,8]{1,0:T(1,128)S(1)} %get-tuple-element.665, f32[1,8]{1,0:T(1,128)S(1)} %get-tuple-element.667, ...), kind=kOutput, calls=%fused_computation.20.clone.1 | convolution fusion | flops 51380320 | bytes 8388737 | tf_op jit(solution)/shard_map/while/body/eval_jaxpr/km,mzxy->kzxy/dot_general | solution.py:103
  199.8 6.5 %all-to-all-start.1 = ((f32[16,4,8,128,8]{3,4,2,1,0:T(8,128)}), f32[16,4,8,128,8]{3,4,2,1,0:T(8,128)S(1)}, u32[]{:S(2)}, u32[]{:S(2)}) async-start(f32[16,4,8,128,8]{3,4,2,1,0:T(8,128)} %copy.139), calls=%async_computation.1 | async-start | bytes 4194304 | tf_op jit(solution)/shard_map/all_to_all | solution.py:52
  208.5 4.2 collective-permute-start.9
  214.0 7.4 %copy.135 = bf16[6,8,8,128,128]{4,3,2,1,0:T(8,128)(2,1)S(1)} copy(bf16[6,8,8,128,128]{4,1,3,2,0:T(8,128)(2,1)} %get-tuple-element.241) | data formatting | bytes 25165824 | tf_op jit(solution)/shard_map/while | solution.py:209
  223.5 4.2 collective-permute-start.2
  229.6 3.9 all-to-all-done.1
  237.2 4.5 all-to-all-start.2
  243.7 7.3 %collective-permute-start.11 = (bf16[24,4,64]{2,1,0:T(4,128)(2,1)S(1)}, bf16[24,4,64]{2,1,0:T(4,128)(2,1)S(1)}, u32[]{:S(2)}, u32[]{:S(2)}) collective-permute-start(bf16[24,4,64]{2,1,0:T(4,128)(2,1)S(1)} %get-tuple-element.531), channel_id=1, source_target_pairs={{1,0},{2,1},{3,2},{4,3},{5,4},{6,5},{7,6},{8,7},{9,8},{10,9},{11,1... | collective-permute-start | bytes 36872 | tf_op jit(solution)/shard_map/ppermute | solution.py:28
  251.0 18.2 %all-to-all-done.2 = f32[8,1,4096]{2,1,0:T(1,128)S(1)} async-done(((f32[8,1,4096]{2,1,0:T(1,128)}), f32[8,1,4096]{2,1,0:T(1,128)S(1)}, u32[]{:S(2)}, u32[]{:S(2)}) %all-to-all-start.2) | async-done | bytes 131104 | tf_op jit(solution)/shard_map/all_to_all | solution.py:246
  275.7 3.9 collective-permute-start.5
  281.3 4.0 collective-permute-done.4
  285.6 3.8 collective-permute-done.5
  292.8 7.4 %collective-permute-start.7 = (bf16[3,24,4,64]{3,2,1,0:T(4,128)(2,1)S(1)}, bf16[3,24,4,64]{3,2,1,0:T(4,128)(2,1)S(1)}, u32[]{:S(2)}, u32[]{:S(2)}) collective-permute-start(bf16[3,24,4,64]{3,2,1,0:T(4,128)(2,1)S(1)} %get-tuple-element.529), channel_id=1, source_target_pairs={{1,0},{2,1},{3,2},{4,3},{5,4},{6,5},{7,6},{8,7},{9,8},{10,9},{11,1... | collective-permute-start | bytes 110600 | tf_op jit(solution)/shard_map/ppermute | solution.py:28
  306.8 3.6 copy.137
  322.3 4.5 all-to-all-start.4
  326.8 13.3 %pad_maximum_fusion.1 = bf16[6,8,10,128,128]{4,1,3,2,0:T(8,128)(2,1)} fusion(bf16[6,8,1,128,128]{4,1,3,2,0:T(8,128)(2,1)} %copy.137, bf16[6,8,8,128,128]{4,1,3,2,0:T(8,128)(2,1)} %get-tuple-element.241, bf16[6,8,1,128,128]{4,1,3,2,0:T(8,128)(2,1)} %copy.136), kind=kLoop, calls=%fused_computation.97 | loop fusion | flops 15728640 | bytes 31457280 | tf_op jit(solution)/shard_map/concatenate | solution.py:24
  342.9 22.1 %all_gather.7 = f32[8,128,128]{1,2,0:T(8,128)} all-gather(f32[8,128,8]{1,2,0:T(8,128)S(1)} %all_to_all.75), channel_id=1, replica_groups=mesh['space'=8,'mode'=16] {'mode'}, dimensions={2}, use_global_device_ids=true | all-gather | bytes 557056 | tf_op jit(solution)/shard_map/all_gather | solution.py:184
  367.1 136.7 %while.29 = (s32[]{:T(128)}, f32[4,8,128,128]{3,0,2,1:T(4,128)}, f32[6,8]{1,0:T(8,128)S(1)}, f32[6,8]{1,0:T(8,128)S(1)}, f32[6,8]{1,0:T(8,128)S(1)}, /*index=5*/...) while((s32[]{:T(128)}, f32[4,8,128,128]{3,0,2,1:T(4,128)}, ...), condition=%wide.region_7.8_spmd.clone, body=%wide.region_6.7_spmd.clone.sunk | while | flops 76808344 | bytes 54527136 | solution.py:209
  373.0 16.9 %select_add_fusion.5 = f32[4,8,128,128]{3,0,2,1:T(4,128)} fusion(f32[4,8,128,128]{3,0,2,1:T(4,128)} %get-tuple-element.739, f32[8,8,128,128]{3,0,2,1:T(8,128)} %slice.1269, f32[8,10,128,128]{3,0,2,1:T(8,128)} %copy-done, f32[8,128,128]{2,1,0:T(8,128)} %get-tuple-element.757, f32[8]{0:T(128)S(1)} %fusion.183, f32[8]{0:T(128)S(1)} %get-tuple-element.683, ...), kind=kOutput, calls=%fused_computation.62.clone.1 | convolution fusion | flops 75497568 | bytes 17301888 | tf_op jit(solution)/shard_map/while/body/eval_jaxpr/km,mzxy->kzxy/dot_general | solution.py:103
  395.8 16.9 %select_add_fusion.5 = f32[4,8,128,128]{3,0,2,1:T(4,128)} fusion(f32[4,8,128,128]{3,0,2,1:T(4,128)} %get-tuple-element.739, f32[8,8,128,128]{3,0,2,1:T(8,128)} %slice.1269, f32[8,10,128,128]{3,0,2,1:T(8,128)} %copy-done, f32[8,128,128]{2,1,0:T(8,128)} %get-tuple-element.757, f32[8]{0:T(128)S(1)} %fusion.183, f32[8]{0:T(128)S(1)} %get-tuple-element.683, ...), kind=kOutput, calls=%fused_computation.62.clone.1 | convolution fusion | flops 75497568 | bytes 17301888 | tf_op jit(solution)/shard_map/while/body/eval_jaxpr/km,mzxy->kzxy/dot_general | solution.py:103
  418.6 16.9 %select_add_fusion.5 = f32[4,8,128,128]{3,0,2,1:T(4,128)} fusion(f32[4,8,128,128]{3,0,2,1:T(4,128)} %get-tuple-element.739, f32[8,8,128,128]{3,0,2,1:T(8,128)} %slice.1269, f32[8,10,128,128]{3,0,2,1:T(8,128)} %copy-done, f32[8,128,128]{2,1,0:T(8,128)} %get-tuple-element.757, f32[8]{0:T(128)S(1)} %fusion.183, f32[8]{0:T(128)S(1)} %get-tuple-element.683, ...), kind=kOutput, calls=%fused_computation.62.clone.1 | convolution fusion | flops 75497568 | bytes 17301888 | tf_op jit(solution)/shard_map/while/body/eval_jaxpr/km,mzxy->kzxy/dot_general | solution.py:103
  441.4 16.9 %select_add_fusion.5 = f32[4,8,128,128]{3,0,2,1:T(4,128)} fusion(f32[4,8,128,128]{3,0,2,1:T(4,128)} %get-tuple-element.739, f32[8,8,128,128]{3,0,2,1:T(8,128)} %slice.1269, f32[8,10,128,128]{3,0,2,1:T(8,128)} %copy-done, f32[8,128,128]{2,1,0:T(8,128)} %get-tuple-element.757, f32[8]{0:T(128)S(1)} %fusion.183, f32[8]{0:T(128)S(1)} %get-tuple-element.683, ...), kind=kOutput, calls=%fused_computation.62.clone.1 | convolution fusion | flops 75497568 | bytes 17301888 | tf_op jit(solution)/shard_map/while/body/eval_jaxpr/km,mzxy->kzxy/dot_general | solution.py:103
  464.1 16.9 %select_add_fusion.5 = f32[4,8,128,128]{3,0,2,1:T(4,128)} fusion(f32[4,8,128,128]{3,0,2,1:T(4,128)} %get-tuple-element.739, f32[8,8,128,128]{3,0,2,1:T(8,128)} %slice.1269, f32[8,10,128,128]{3,0,2,1:T(8,128)} %copy-done, f32[8,128,128]{2,1,0:T(8,128)} %get-tuple-element.757, f32[8]{0:T(128)S(1)} %fusion.183, f32[8]{0:T(128)S(1)} %get-tuple-element.683, ...), kind=kOutput, calls=%fused_computation.62.clone.1 | convolution fusion | flops 75497568 | bytes 17301888 | tf_op jit(solution)/shard_map/while/body/eval_jaxpr/km,mzxy->kzxy/dot_general | solution.py:103
  486.9 16.9 %select_add_fusion.5 = f32[4,8,128,128]{3,0,2,1:T(4,128)} fusion(f32[4,8,128,128]{3,0,2,1:T(4,128)} %get-tuple-element.739, f32[8,8,128,128]{3,0,2,1:T(8,128)} %slice.1269, f32[8,10,128,128]{3,0,2,1:T(8,128)} %copy-done, f32[8,128,128]{2,1,0:T(8,128)} %get-tuple-element.757, f32[8]{0:T(128)S(1)} %fusion.183, f32[8]{0:T(128)S(1)} %get-tuple-element.683, ...), kind=kOutput, calls=%fused_computation.62.clone.1 | convolution fusion | flops 75497568 | bytes 17301888 | tf_op jit(solution)/shard_map/while/body/eval_jaxpr/km,mzxy->kzxy/dot_general | solution.py:103
  508.6 32.3 %all_to_all.88 = f32[16,4,8,128,8]{3,4,2,1,0:T(8,128)} all-to-all(f32[16,4,8,128,8]{3,4,2,1,0:T(8,128)S(1)} %copy.152), channel_id=1, replica_groups=mesh['space'=8,'mode'=16] {'mode'}, dimensions={0} | all-to-all | bytes 4194304 | tf_op jit(solution)/shard_map/all_to_all | solution.py:52
  548.2 10.1 %all_to_all.89 = f32[8,1,4096]{2,1,0:T(1,128)S(1)} all-to-all(f32[8,1,4096]{2,1,0:T(1,128)S(1)} %reshape.256), channel_id=1, replica_groups=mesh['space'=8,'mode'=16] {'space'}, dimensions={0} | all-to-all | bytes 262144 | tf_op jit(solution)/shard_map/all_to_all | solution.py:246
  567.4 3.8 collective-permute-start.12
  574.2 5.2 collective-permute-done.12
  580.7 4.3 collective-permute-done.13
  589.2 7.5 %collective-permute-start.15 = (bf16[3,24,4,64]{3,2,1,0:T(4,128)(2,1)S(1)}, bf16[3,24,4,64]{3,2,1,0:T(4,128)(2,1)}, u32[]{:S(2)}, u32[]{:S(2)}) collective-permute-start(bf16[3,24,4,64]{3,2,1,0:T(4,128)(2,1)S(1)} %get-tuple-element.527), channel_id=1, source_target_pairs={{1,0},{2,1},{3,2},{4,3},{5,4},{6,5},{7,6},{8,7},{9,8},{10,9},{11,1... | collective-permute-start | bytes 110600 | tf_op jit(solution)/shard_map/ppermute | solution.py:28
  (258 shorter events, 170.3 us)
Async XLA Ops:
  0.6 9.9 %copy-start.4 = (f32[16,8,64]{2,1,0:T(8,128)S(1)}, f32[16,8,64]{2,1,0:T(8,128)}, u32[]{:S(2)}) copy-start(f32[16,8,64]{2,1,0:T(8,128)} %param.14) | copy-start | bytes 98308
  0.6 17.6 %copy-start.11 = (s32[48]{0:T(128)S(1)}, s32[48]{0:T(128)}, u32[]{:S(2)}) copy-start(s32[48]{0:T(128)} %param.17) | copy-start | bytes 580
  0.7 17.6 %copy-start.10 = (f32[6]{0:T(128)S(1)}, f32[6]{0:T(128)}, u32[]{:S(2)}) copy-start(f32[6]{0:T(128)} %param.19) | copy-start | bytes 76
  0.7 17.7 %copy-start.7 = (s32[48]{0:T(128)S(1)}, s32[48]{0:T(128)}, u32[]{:S(2)}) copy-start(s32[48]{0:T(128)} %param.18) | copy-start | bytes 580
  0.7 17.8 %copy-start.8 = (f32[48]{0:T(128)S(1)}, f32[48]{0:T(128)}, u32[]{:S(2)}) copy-start(f32[48]{0:T(128)} %param.15) | copy-start | bytes 580
  0.7 17.8 %copy-start.9 = (f32[48]{0:T(128)S(1)}, f32[48]{0:T(128)}, u32[]{:S(2)}) copy-start(f32[48]{0:T(128)} %param.16) | copy-start | bytes 580
  4.7 77.6 %collective-permute-start = (bf16[48,1,128,128]{3,2,1,0:T(8,128)(2,1)}, bf16[48,1,128,128]{3,2,1,0:T(8,128)(2,1)}, u32[]{:S(2)}, u32[]{:S(2)}) collective-permute-start(bf16[48,1,128,128]{3,2,1,0:T(8,128)(2,1)} %get-tuple-element.508), channel_id=1, source_target_pairs={{0,16},{16,32},{32,48},{48,64},{64,80},{80,96},{96,112},{1,17},{17... | collective-permute-start | bytes 4718600 | tf_op jit(solution)/shard_map/ppermute | solution.py:26
  8.1 74.2 %collective-permute-start.1 = (bf16[48,1,128,128]{3,2,1,0:T(8,128)(2,1)}, bf16[48,1,128,128]{3,2,1,0:T(8,128)(2,1)}, u32[]{:S(2)}, u32[]{:S(2)}) collective-permute-start(bf16[48,1,128,128]{3,2,1,0:T(8,128)(2,1)} %get-tuple-element.509), channel_id=1, source_target_pairs={{16,0},{32,16},{48,32},{64,48},{80,64},{96,80},{112,96},{17,1},{33... | collective-permute-start | bytes 4718600 | tf_op jit(solution)/shard_map/ppermute | solution.py:28
  11.5 37.1 %all-to-all-start = ((f32[8,1,1024]{2,1,0:T(1,128)}), f32[8,1,1024]{2,1,0:T(1,128)S(1)}, u32[]{:S(2)}, u32[]{:S(2)}) async-start(f32[8,1,1024]{2,1,0:T(1,128)} %reshape.250), calls=%async_computation | async-start | bytes 65536 | tf_op jit(solution)/shard_map/all_to_all | solution.py:183
  49.9 149.9 %all-to-all-start.3 = ((f32[16,1,1]{2,1,0:T(1,128)}), f32[16,1,1]{2,1,0:T(1,128)S(1)}, u32[]{:S(2)}, u32[]{:S(2)}) async-start(f32[16,1,1]{2,1,0:T(1,128)} %broadcast_in_dim.52), calls=%async_computation.3 | async-start | bytes 16384 | tf_op jit(solution)/shard_map/all_to_all | solution.py:37
  196.5 9.8 %copy-start.5 = (f32[16,8,64]{2,1,0:T(8,128)S(1)}, f32[16,8,64]{2,1,0:T(8,128)}, u32[]{:S(2)}) copy-start(f32[16,8,64]{2,1,0:T(8,128)} %param.20) | copy-start | bytes 98308
  196.5 9.8 %copy-start.6 = (s32[16,8,64]{2,1,0:T(8,128)S(1)}, s32[16,8,64]{2,1,0:T(8,128)}, u32[]{:S(2)}) copy-start(s32[16,8,64]{2,1,0:T(8,128)} %param.21) | copy-start | bytes 98308
  199.8 33.8 %all-to-all-start.1 = ((f32[16,4,8,128,8]{3,4,2,1,0:T(8,128)}), f32[16,4,8,128,8]{3,4,2,1,0:T(8,128)S(1)}, u32[]{:S(2)}, u32[]{:S(2)}) async-start(f32[16,4,8,128,8]{3,4,2,1,0:T(8,128)} %copy.139), calls=%async_computation.1 | async-start | bytes 4194304 | tf_op jit(solution)/shard_map/all_to_all | solution.py:52
  206.4 23.2 %collective-permute-start.8 = (bf16[4,8,64]{2,1,0:T(8,128)(2,1)S(1)}, bf16[4,8,64]{2,1,0:T(8,128)(2,1)S(1)}, u32[]{:S(2)}, u32[]{:S(2)}) collective-permute-start(bf16[4,8,64]{2,1,0:T(8,128)(2,1)S(1)} %get-tuple-element.532), channel_id=1, source_target_pairs={{0,16},{16,32},{32,48},{48,64},{64,80},{80,96},{96,112},{1,17},{17... | collective-permute-start | bytes 12296 | tf_op jit(solution)/shard_map/ppermute | solution.py:26
  208.5 21.1 %collective-permute-start.9 = (bf16[4,8,64]{2,1,0:T(8,128)(2,1)S(1)}, bf16[4,8,64]{2,1,0:T(8,128)(2,1)S(1)}, u32[]{:S(2)}, u32[]{:S(2)}) collective-permute-start(bf16[4,8,64]{2,1,0:T(8,128)(2,1)S(1)} %get-tuple-element.533), channel_id=1, source_target_pairs={{16,0},{32,16},{48,32},{64,48},{80,64},{96,80},{112,96},{17,1},{33... | collective-permute-start | bytes 12296 | tf_op jit(solution)/shard_map/ppermute | solution.py:28
  223.5 79.8 %collective-permute-start.2 = (bf16[48,1,128,128]{3,2,1,0:T(8,128)(2,1)}, bf16[48,1,128,128]{3,2,1,0:T(8,128)(2,1)}, u32[]{:S(2)}, u32[]{:S(2)}) collective-permute-start(bf16[48,1,128,128]{3,2,1,0:T(8,128)(2,1)} %get-tuple-element.506), channel_id=1, source_target_pairs={{0,16},{16,32},{32,48},{48,64},{64,80},{80,96},{96,112},{1,17},{17... | collective-permute-start | bytes 4718600 | tf_op jit(solution)/shard_map/ppermute | solution.py:26
  227.7 79.2 %collective-permute-start.3 = (bf16[48,1,128,128]{3,2,1,0:T(8,128)(2,1)}, bf16[48,1,128,128]{3,2,1,0:T(8,128)(2,1)}, u32[]{:S(2)}, u32[]{:S(2)}) collective-permute-start(bf16[48,1,128,128]{3,2,1,0:T(8,128)(2,1)} %get-tuple-element.507), channel_id=1, source_target_pairs={{16,0},{32,16},{48,32},{64,48},{80,64},{96,80},{112,96},{17,1},{33... | collective-permute-start | bytes 4718600 | tf_op jit(solution)/shard_map/ppermute | solution.py:28
  237.2 32.0 %all-to-all-start.2 = ((f32[8,1,4096]{2,1,0:T(1,128)}), f32[8,1,4096]{2,1,0:T(1,128)S(1)}, u32[]{:S(2)}, u32[]{:S(2)}) async-start(f32[8,1,4096]{2,1,0:T(1,128)} %reshape.252), calls=%async_computation.2 | async-start | bytes 262144 | tf_op jit(solution)/shard_map/all_to_all | solution.py:246
  241.8 33.9 %collective-permute-start.10 = (bf16[24,4,64]{2,1,0:T(4,128)(2,1)S(1)}, bf16[24,4,64]{2,1,0:T(4,128)(2,1)S(1)}, u32[]{:S(2)}, u32[]{:S(2)}) collective-permute-start(bf16[24,4,64]{2,1,0:T(4,128)(2,1)S(1)} %get-tuple-element.530), channel_id=1, source_target_pairs={{0,1},{1,2},{2,3},{3,4},{4,5},{5,6},{6,7},{7,8},{8,9},{9,10},{10,1... | collective-permute-start | bytes 36872 | tf_op jit(solution)/shard_map/ppermute | solution.py:26
  243.7 35.9 %collective-permute-start.11 = (bf16[24,4,64]{2,1,0:T(4,128)(2,1)S(1)}, bf16[24,4,64]{2,1,0:T(4,128)(2,1)S(1)}, u32[]{:S(2)}, u32[]{:S(2)}) collective-permute-start(bf16[24,4,64]{2,1,0:T(4,128)(2,1)S(1)} %get-tuple-element.531), channel_id=1, source_target_pairs={{1,0},{2,1},{3,2},{4,3},{5,4},{6,5},{7,6},{8,7},{9,8},{10,9},{11,1... | collective-permute-start | bytes 36872 | tf_op jit(solution)/shard_map/ppermute | solution.py:28
  272.4 20.4 %copy-start.2 = (f32[4,8,8,16,8]{3,4,2,1,0:T(8,128)}, f32[4,8,8,16,8]{3,4,2,1,0:T(8,128)S(1)}, u32[]{:S(2)}) copy-start(f32[4,8,8,16,8]{3,4,2,1,0:T(8,128)S(1)} %copy.142) | copy-start | bytes 393220
  273.7 11.6 %collective-permute-start.4 = (bf16[3,4,8,64]{1,2,3,0:T(8,128)(2,1)}, bf16[3,4,8,64]{1,2,3,0:T(8,128)(2,1)S(1)}, u32[]{:S(2)}, u32[]{:S(2)}) collective-permute-start(bf16[3,4,8,64]{1,2,3,0:T(8,128)(2,1)} %get-tuple-element.522), channel_id=1, source_target_pairs={{0,16},{16,32},{32,48},{48,64},{64,80},{80,96},{96,112},{1,17},{17... | collective-permute-start | bytes 36872 | tf_op jit(solution)/shard_map/ppermute | solution.py:26
  275.7 13.8 %collective-permute-start.5 = (bf16[3,4,8,64]{1,2,3,0:T(8,128)(2,1)}, bf16[3,4,8,64]{1,2,3,0:T(8,128)(2,1)}, u32[]{:S(2)}, u32[]{:S(2)}) collective-permute-start(bf16[3,4,8,64]{1,2,3,0:T(8,128)(2,1)} %get-tuple-element.523), channel_id=1, source_target_pairs={{16,0},{32,16},{48,32},{64,48},{80,64},{96,80},{112,96},{17,1},{33... | collective-permute-start | bytes 36872 | tf_op jit(solution)/shard_map/ppermute | solution.py:28
  290.9 19.6 %collective-permute-start.6 = (bf16[3,24,4,64]{3,2,1,0:T(4,128)(2,1)S(1)}, bf16[3,24,4,64]{3,2,1,0:T(4,128)(2,1)S(1)}, u32[]{:S(2)}, u32[]{:S(2)}) collective-permute-start(bf16[3,24,4,64]{3,2,1,0:T(4,128)(2,1)S(1)} %get-tuple-element.528), channel_id=1, source_target_pairs={{0,1},{1,2},{2,3},{3,4},{4,5},{5,6},{6,7},{7,8},{8,9},{9,10},{10,1... | collective-permute-start | bytes 110600 | tf_op jit(solution)/shard_map/ppermute | solution.py:26
  292.8 17.6 %collective-permute-start.7 = (bf16[3,24,4,64]{3,2,1,0:T(4,128)(2,1)S(1)}, bf16[3,24,4,64]{3,2,1,0:T(4,128)(2,1)S(1)}, u32[]{:S(2)}, u32[]{:S(2)}) collective-permute-start(bf16[3,24,4,64]{3,2,1,0:T(4,128)(2,1)S(1)} %get-tuple-element.529), channel_id=1, source_target_pairs={{1,0},{2,1},{3,2},{4,3},{5,4},{6,5},{7,6},{8,7},{9,8},{10,9},{11,1... | collective-permute-start | bytes 110600 | tf_op jit(solution)/shard_map/ppermute | solution.py:28
  313.5 1.0 copy-start.1
  322.3 17.9 %all-to-all-start.4 = ((f32[8,1,1024]{2,1,0:T(1,128)}), f32[8,1,1024]{2,1,0:T(1,128)S(1)}, u32[]{:S(2)}, u32[]{:S(2)}) async-start(f32[8,1,1024]{2,1,0:T(1,128)} %reshape.254), calls=%async_computation.4 | async-start | bytes 65536 | tf_op jit(solution)/shard_map/all_to_all | solution.py:183
  369.3 3.7 copy-start
  392.1 3.7 copy-start
  414.9 3.7 copy-start
  437.7 3.7 copy-start
  460.5 3.7 copy-start
  483.3 3.7 copy-start
  567.4 12.0 %collective-permute-start.12 = (bf16[3,4,8,64]{1,2,3,0:T(8,128)(2,1)}, bf16[3,4,8,64]{1,2,3,0:T(8,128)(2,1)}, u32[]{:S(2)}, u32[]{:S(2)}) collective-permute-start(bf16[3,4,8,64]{1,2,3,0:T(8,128)(2,1)} %get-tuple-element.524), channel_id=1, source_target_pairs={{0,16},{16,32},{32,48},{48,64},{64,80},{80,96},{96,112},{1,17},{17... | collective-permute-start | bytes 36872 | tf_op jit(solution)/shard_map/ppermute | solution.py:26
  571.3 13.7 %collective-permute-start.13 = (bf16[3,4,8,64]{1,2,3,0:T(8,128)(2,1)}, bf16[3,4,8,64]{1,2,3,0:T(8,128)(2,1)}, u32[]{:S(2)}, u32[]{:S(2)}) collective-permute-start(bf16[3,4,8,64]{1,2,3,0:T(8,128)(2,1)} %get-tuple-element.525), channel_id=1, source_target_pairs={{16,0},{32,16},{48,32},{64,48},{80,64},{96,80},{112,96},{17,1},{33... | collective-permute-start | bytes 36872 | tf_op jit(solution)/shard_map/ppermute | solution.py:28
  587.3 13.6 %collective-permute-start.14 = (bf16[3,24,4,64]{3,2,1,0:T(4,128)(2,1)S(1)}, bf16[3,24,4,64]{3,2,1,0:T(4,128)(2,1)S(1)}, u32[]{:S(2)}, u32[]{:S(2)}) collective-permute-start(bf16[3,24,4,64]{3,2,1,0:T(4,128)(2,1)S(1)} %get-tuple-element.526), channel_id=1, source_target_pairs={{0,1},{1,2},{2,3},{3,4},{4,5},{5,6},{6,7},{7,8},{8,9},{9,10},{10,1... | collective-permute-start | bytes 110600 | tf_op jit(solution)/shard_map/ppermute | solution.py:26
  589.2 12.3 %collective-permute-start.15 = (bf16[3,24,4,64]{3,2,1,0:T(4,128)(2,1)S(1)}, bf16[3,24,4,64]{3,2,1,0:T(4,128)(2,1)}, u32[]{:S(2)}, u32[]{:S(2)}) collective-permute-start(bf16[3,24,4,64]{3,2,1,0:T(4,128)(2,1)S(1)} %get-tuple-element.527), channel_id=1, source_target_pairs={{1,0},{2,1},{3,2},{4,3},{5,4},{6,5},{7,6},{8,7},{9,8},{10,9},{11,1... | collective-permute-start | bytes 110600 | tf_op jit(solution)/shard_map/ppermute | solution.py:28
  600.9 0.6 copy-start.3
where the time goes:
time: 627 us; the launch traced here: 615 us
  matrix products  143 us (23%)
  local copies, waits for them, and re-layouts  113 us (18%)
  other arithmetic  111 us (18%)
  starting transfers between devices  87.7 us (14%)
  blocking collectives  87.6 us (14%)
  waiting for transfers between devices  68.6 us (11%)
    dot_general x12, matrix products, upwind(): jnp.einsum('km,mzxy->kzxy', weights, updated, precision=lax.Precision.HIG...  143 us
    all_gather x2, blocking collectives, to_slab(): return lax.all_gather(moved, 'mode', axis=2, tiled=True)  45.2 us
    ppermute x8, starting transfers between devices, padded_2(): lax.ppermute(head, axis, [((i + 1) % count, i) for i in range(ends)])  36.6 us
    all_to_all x1, blocking collectives, sum_at_owner(): lax.all_to_all(in_blocks(shard, dim, length), axis, 0, 0, tiled=True)  32.3 us
    dynamic_update_slice x6, other arithmetic, kinetic(): moments, news = lax.scan(step, start, (shaped,) + params)  31.9 us
    all_to_all x2, waiting for transfers between devices, to_slab(): lax.all_to_all(upright, 'space', split_axis=0, concat_axis=1, tiled=True)  29.1 us
    concatenate x8, other arithmetic, padded_2(): jnp.concatenate([lax.ppermute(tail, axis, [(i, (i + 1) % count) for i in...  29 us
    convert_element_type x12, other arithmetic, step(): block.astype(jnp.float32)  23.6 us
  transfers between devices with their start and end apart: 21, of which 7 were waited for; matrix products, arithmetic and copies ran while one was open for 28% of the time, Pallas kernels for 0%

commit v1 on v0

v1 whole, which is shorter than its diff:
```python
import math

import jax
import jax.numpy as jnp
from jax import lax
from jax.experimental import pallas as pl
from jax.experimental.pallas import tpu as pltpu
from jax.sharding import Mesh, PartitionSpec as P


SWEEPS = 4
STEP = 0.25
MODES = 768
LOCAL = 48
SLAB = 8
NX = 128
NY = 128
WIN = 5 * LOCAL
DEPTH = 256
EXT = 12
PITCH = 17
ROWS = 6 * EXT * 8
PIECE = ROWS + 16
F32 = jnp.float32
BF16 = jnp.bfloat16

SHIFTS = (
    (0, 0), (1, 0), (-1, 0), (2, 0), (-2, 0),
    (0, 1), (1, 1), (-1, 1),
    (0, -1), (1, -1), (-1, -1),
    (0, 2), (0, -2),
)
NS = len(SHIFTS)
BY_Z = tuple(
    (sz, tuple((sy, n) for n, (sy, z) in enumerate(SHIFTS) if z == sz)) for sz in (-2, -1, 0, 1, 2)
)


def lane_iota(shape):
    return lax.broadcasted_iota(jnp.int32, shape, len(shape) - 1)


def mode_rows(table, prop_ref):
    branch = table[0:1]
    orient = table[1:2]
    cap = table[2:3] / float(MODES)
    rate = 1.0 / table[3:4]
    speed = jnp.zeros_like(branch)
    for b in range(6):
        speed = speed + jnp.where(branch == float(b), prop_ref[b], 0.0)
    polar = jnp.where(orient >= 4.0, 1.0, 0.0) + jnp.where(orient >= 8.0, 1.0, 0.0)
    polar = polar + jnp.where(orient >= 12.0, 1.0, 0.0)
    turn = orient - 4.0 * polar
    cosine = (2.0 * polar + 1.0) * 0.25 - 1.0
    sine = jnp.sqrt(1.0 - cosine * cosine)
    half = math.sqrt(0.5)
    east = jnp.where((turn == 0.0) | (turn == 3.0), half, -half)
    north = jnp.where(turn < 2.0, half, -half)
    return speed * sine * east, speed * sine * north, speed * cosine, rate, cap


def step_terms(vx, vy, vz, rate):
    cx, cy, cz = (STEP * jnp.abs(v) for v in (vx, vy, vz))
    c0 = 1.0 - cx - cy - cz - STEP * rate
    one = (((0, 0, 0), c0), ((1, 0, 0), cx), ((0, 1, 0), cy), ((0, 0, 1), cz))
    two = (
        ((0, 0, 0), c0 * c0),
        ((1, 0, 0), 2.0 * c0 * cx),
        ((0, 1, 0), 2.0 * c0 * cy),
        ((0, 0, 1), 2.0 * c0 * cz),
        ((2, 0, 0), cx * cx),
        ((0, 2, 0), cy * cy),
        ((0, 0, 2), cz * cz),
        ((1, 1, 0), 2.0 * cx * cy),
        ((1, 0, 1), 2.0 * cx * cz),
        ((0, 1, 1), 2.0 * cy * cz),
    )
    return one, two


def fields_on_rows(vx, vy, vz, rate):
    lanes = rate.shape[1]
    row = lax.broadcasted_iota(jnp.int32, (8, lanes), 0) % 4
    full = [jnp.broadcast_to(v, (8, lanes)) for v in (rate, vx, vy, vz)]
    return jnp.where(
        row == 0, full[0], jnp.where(row == 1, full[1], jnp.where(row == 2, full[2], full[3]))
    )


def build_tables(par_ref, prop_ref, par5, coef):
    par5[...] = jnp.ones(par5.shape, F32)
    for o in range(5):
        par5[0:4, o * LOCAL : (o + 1) * LOCAL] = par_ref[...]
    vx, vy, vz, rate, _ = mode_rows(par5[0:4, :], prop_ref)
    one, two = step_terms(vx, vy, vz, rate)
    weights = fields_on_rows(vx, vy, vz, rate)
    lane = lane_iota((1, DEPTH))
    offset = -2.0 + sum(jnp.where(lane >= o * LOCAL, 1.0, 0.0) for o in range(1, 5))
    inside = lane < WIN
    dx, dy, dz = (jnp.where(v > 0.0, 1.0, -1.0) for v in (vx, vy, vz))
    upper = lax.broadcasted_iota(jnp.int32, (8, DEPTH), 0) < 4

    def total(terms, sy, sz):
        out = jnp.zeros((1, DEPTH), F32)
        for (ax, ay, az), value in terms:
            if ay != abs(sy) or az != abs(sz):
                continue
            hit = inside & (offset == -float(ax) * dx)
            if ay:
                hit = hit & (dy * float(ay) == float(sy))
            if az:
                hit = hit & (dz * float(az) == float(sz))
            out = out + jnp.where(hit, value, 0.0)
        return jnp.broadcast_to(out, (8, DEPTH))

    parts = [
        weights * jnp.where(upper, total(one, sy, sz), total(two, sy, sz)) for sy, sz in SHIFTS
    ]
    rest = parts[0] - parts[0].astype(BF16).astype(F32)
    coef[...] = jnp.concatenate(parts + [rest], axis=0).astype(BF16)


def mode_sums(par_ref, prop_ref, core):
    vx, vy, vz, rate, cap = mode_rows(par_ref[...], prop_ref)
    one, _ = step_terms(vx, vy, vz, rate)
    weights = fields_on_rows(vx, vy, vz, rate)
    gain = STEP * rate * cap
    columns = [weights * gain * one[0][1]]
    for ((ax, ay, az), value), v in zip(one[1:], (vx, vy, vz)):
        for sign in (1.0, -1.0):
            columns.append(weights * gain * jnp.where(v * sign > 0.0, value, 0.0))
    columns.append(weights * gain)
    columns.append(jnp.broadcast_to(cap * rate, weights.shape))
    lane = lane_iota((8, 128))
    sums = jnp.zeros((8, 128), F32)
    for n, column in enumerate(columns):
        sums = jnp.where(lane == n, jnp.sum(column, axis=1, keepdims=True), sums)
    high = sums.astype(BF16).astype(F32)
    rest = sums - high
    middle = rest.astype(BF16).astype(F32)
    low = rest - middle
    packed = high + pltpu.roll(middle, 16, 1) + pltpu.roll(low, 32, 1)
    packed = jnp.where(core == 0, packed, pltpu.roll(packed, 64, 1))
    return jnp.concatenate([packed, jnp.zeros((8, 128), F32)], axis=0).astype(BF16)


def moments_kernel(idx_ref, prop_ref, par_ref, e_ref, keep_ref, send_ref, par5, coef, spread, turned, acc):
    z = pl.program_id(0)
    space = idx_ref[0]
    core = idx_ref[1]
    LAYER = NX * 8

    @pl.when(z == 0)
    def _():
        build_tables(par_ref, prop_ref, par5, coef)
        turned[0 : 2 * LOCAL, :] = jnp.zeros((2 * LOCAL, 128), BF16)
        turned[(NX + 2) * LOCAL :, :] = jnp.zeros((2 * LOCAL + 16, 128), BF16)

        @pl.loop(0, 5 * LAYER // 64)
        def _(r):
            acc[pl.ds(pl.multiple_of(r * 64, 64), 64), :] = jnp.zeros((64, 128), F32)

        acc[13 * LAYER : 14 * LAYER, :] = jnp.zeros((LAYER, 128), F32)

    @pl.loop(0, NX // 16)
    def _(c):
        x0 = pl.multiple_of(c * 16, 16)
        for m in range(LOCAL):
            spread[m * PITCH : m * PITCH + 16, :] = e_ref[m, 0, pl.ds(x0, 16), :].astype(F32)
        for xx in range(16):
            rows = spread[pl.ds(xx, LOCAL, stride=PITCH), :].astype(BF16)
            turned[pl.ds(pl.multiple_of((x0 + (xx + 2)) * LOCAL, 16), LOCAL), :] = rows

    lane = lane_iota((8, 128))

    def moved(value, sy):
        if sy == 0:
            return value
        rolled = pltpu.roll(value, sy % 128, 1)
        return jnp.where(lane >= sy if sy > 0 else lane < 128 + sy, rolled, 0.0)

    def one_pair(x):
            first = turned[x * LOCAL : x * LOCAL + DEPTH, :]
            second = turned[(x + 1) * LOCAL : (x + 1) * LOCAL + DEPTH, :]
            block = jnp.concatenate([first, second], axis=1)
            out = jnp.dot(coef[...], block, preferred_element_type=F32)
            for half in range(2):
                for sz, members in BY_Z:
                    total = None
                    for sy, n in members:
                        part = moved(out[8 * n : 8 * n + 8, 128 * half : 128 * half + 128], sy)
                        if n == 0:
                            part = part + out[8 * NS :, 128 * half : 128 * half + 128]
                        total = part if total is None else total + part
                    at = pl.multiple_of((z + 3 + sz) * LAYER + (x + half) * 8, 8)
                    if sz == 2:
                        acc[pl.ds(at, 8), :] = total
                    else:
                        acc[pl.ds(at, 8), :] += total

    for x in range(0, NX, 2):
        one_pair(x)

    @pl.when(z == SLAB - 1)
    def _():
        @pl.when(space == 0)
        def _():
            acc[LAYER : 3 * LAYER, :] = jnp.zeros((2 * LAYER, 128), F32)

        @pl.when(space == 7)
        def _():
            acc[11 * LAYER : 13 * LAYER, :] = jnp.zeros((2 * LAYER, 128), F32)

        def give(ref, block, at, tile):
            ref[block, pl.ds(at, 16), :] = tile.astype(ref.dtype)

        row = lax.broadcasted_iota(jnp.int32, (NX, 128), 0)
        col = lane_iota((NX, 128))

        def layer(zo, field, shift=0):
            return acc[pl.ds((zo + 1) * LAYER + field + 8 * shift, NX, stride=8), :]

        def divergence(zo):
            east = jnp.where(row < NX - 1, layer(zo, 1, 1), 0.0)
            west = jnp.where(row > 0, layer(zo, 1, -1), 0.0)
            along_y = layer(zo, 2)
            north = jnp.where(col < 127, pltpu.roll(along_y, 127, 1), 0.0)
            south = jnp.where(col > 0, pltpu.roll(along_y, 1, 1), 0.0)
            up = layer(zo + 1, 3)
            down = layer(zo - 1, 3)
            return 0.5 * ((east - west) + (north - south) + (up - down))

        sources = (
            lambda zo: layer(zo, 0),
            divergence,
            lambda zo: layer(zo, 5),
            lambda zo: layer(zo, 6),
            lambda zo: layer(zo, 7),
            lambda zo: layer(zo, 4),
        )
        for f, source in enumerate(sources):

            @pl.loop(0, EXT // 2)
            def _(pair):
                zo = pair * 2
                even = source(zo).T
                odd = source(zo + 1).T
                at = pl.multiple_of((f * EXT + zo) * 8, 16)
                tiles = [
                    jnp.concatenate([even[8 * j : 8 * j + 8], odd[8 * j : 8 * j + 8]], axis=0)
                    for j in range(16)
                ]

                @pl.when(core == 0)
                def _():
                    for j in range(16):
                        give(send_ref if j % 2 else keep_ref, j // 2, at, tiles[j])

                @pl.when(core == 1)
                def _():
                    for j in range(16):
                        give(keep_ref if j % 2 else send_ref, j // 2, at, tiles[j])

        sums = mode_sums(par_ref, prop_ref, core)
        for p in range(8):
            keep_ref[p, ROWS:PIECE, :] = sums.astype(F32)
            send_ref[p, ROWS:PIECE, :] = sums


def moments(idx, prop, par, state):
    whole = pl.BlockSpec((8, PIECE, 128), lambda z: (0, 0, 0))
    return pl.pallas_call(
        moments_kernel,
        grid=(SLAB,),
        in_specs=[
            pl.BlockSpec(memory_space=pltpu.SMEM),
            pl.BlockSpec(memory_space=pltpu.SMEM),
            pl.BlockSpec((4, LOCAL), lambda z: (0, 0)),
            pl.BlockSpec((LOCAL, 1, NX, NY), lambda z: (0, z, 0, 0)),
        ],
        out_specs=[whole, whole],
        out_shape=[jax.ShapeDtypeStruct((8, PIECE, 128), t) for t in (F32, BF16)],
        scratch_shapes=[
            pltpu.VMEM((8, DEPTH), F32),
            pltpu.VMEM((NS * 8 + 8, DEPTH), BF16),
            pltpu.VMEM((LOCAL * PITCH + 8, 128), F32),
            pltpu.VMEM(((NX + 4) * LOCAL + 16, 128), BF16),
            pltpu.VMEM((14 * NX * 8, 128), F32),
        ],
        compiler_params=pltpu.CompilerParams(vmem_limit_bytes=48 << 20),
        cost_estimate=pl.CostEstimate(flops=20_000_000_000, bytes_accessed=16_000_000, transcendentals=0),
        name="moments",
    )(idx, prop, par, state)


def owner_kernel(got_ref, out_ref, sums_ref):
    lane = lane_iota((8, 128))
    part = lane % 32
    for f in range(6):
        for high in range(EXT // 4):
            base = (f * EXT + high * 4) * 8
            layers = got_ref[0, base : base + 32, :].astype(F32)
            for m in range(1, 8):
                layers = layers + got_ref[m, base : base + 32, :].astype(F32)
            tiles = []
            for i in range(8):
                value = None
                for low in range(4):
                    rolled = pltpu.roll(layers[8 * low : 8 * low + 8], (32 * low - 16 * i + 8) % 128, 1)
                    value = rolled if low == 0 else jnp.where(lane >= 32 * low, rolled, value)
                if i == 0:
                    value = jnp.where(part >= 8, value, 0.0)
                if i == 7:
                    value = jnp.where(part < 24, value, 0.0)
                tiles.append(value)
            at = (f * 3 + high) * 8
            for i in range(8):
                out_ref[i, at : at + 8, :] = tiles[i].astype(BF16)
                if f in (2, 3, 4):
                    low = tiles[i] - tiles[i].astype(BF16).astype(F32)
                    out_ref[i, at + 96 : at + 104, :] = low.astype(BF16)
    total = got_ref[0, ROWS:PIECE, :].astype(F32)
    for m in range(1, 8):
        total = total + got_ref[m, ROWS:PIECE, :].astype(F32)
    total = total[0:8]
    total = total + pltpu.roll(total, 64, 1)
    sums_ref[...] = total + pltpu.roll(total, 112, 1) + pltpu.roll(total, 96, 1)


def at_owner(got):
    return pl.pallas_call(
        owner_kernel,
        out_shape=[
            jax.ShapeDtypeStruct((8, 216, 128), BF16),
            jax.ShapeDtypeStruct((8, 128), F32),
        ],
        name="owner",
    )(got)


def merge_kernel(got_ref, known_ref, own_ref, halo_ref):
    group = lane_iota((8, 128)) // 32

    def layer(s, f, zo, quarter):
        at = (f * 3 + zo // 4) * 8
        value = got_ref[s, at : at + 8, :].astype(F32)
        if f in (2, 3, 4):
            value = value + got_ref[s, at + 96 : at + 104, :].astype(F32)
        turn = (32 * (quarter - zo % 4)) % 128
        return pltpu.roll(value, turn, 1) if turn else value

    for f in range(6):
        for zz in range(16):
            value = None
            for quarter in range(4):
                z = quarter * 16 + zz
                s = z // 8
                part = layer(s, f, z % 8 + 2, quarter)
                if z % 8 < 2 and s > 0:
                    part = part + layer(s - 1, f, z % 8 + 10, quarter)
                if z % 8 > 5 and s < 7:
                    part = part + layer(s + 1, f, z % 8 - 6, quarter)
                value = part if quarter == 0 else jnp.where(group >= quarter, part, value)
            own_ref[f, zz] = value
            if f < 5:
                halo_ref[(f * 16 + zz) * 8 : (f * 16 + zz) * 8 + 8, :] = value.astype(BF16)
    for n in range(2):
        halo_ref[640 + 128 * n : 768 + 128 * n, :] = known_ref[n].reshape(128, 128).astype(BF16)


def merged(got, known):
    return pl.pallas_call(
        merge_kernel,
        out_shape=[
            jax.ShapeDtypeStruct((6, 16, 8, 128), F32),
            jax.ShapeDtypeStruct((7 * 16 * 8, 128), BF16),
        ],
        name="merge",
    )(got, known)


def solve_kernel(idx_ref, sums_ref, own_ref, south_ref, north_ref, known_ref, temp_ref, flux_ref):
    lane = lane_iota((1, 24, 128))
    x = lane % 32 + (idx_ref[0] * 16 - 8)
    y = lax.broadcasted_iota(jnp.int32, (1, 24, 128), 1) + (idx_ref[1] * 8 - 8)
    inside = jnp.where((x >= 0) & (x < NX) & (y >= 0) & (y < NY), 1.0, 0.0)
    group = lane_iota((1, 24, 128)) // 32

    def wide(own, f):
        rows = slice(f * 128, f * 128 + 128)
        south = south_ref[rows, :].astype(F32).reshape(16, 8, 128)
        north = north_ref[rows, :].astype(F32).reshape(16, 8, 128)
        return jnp.concatenate([south, own, north], axis=1)

    def field(f):
        return wide(own_ref[f], f)

    def known(n):
        return wide(known_ref[n], 5 + n)

    def east(v):
        return pltpu.roll(v, 127, 2)

    def west(v):
        return pltpu.roll(v, 1, 2)

    def north(v):
        return jnp.concatenate([v[:, 1:], jnp.zeros((16, 1, 128), F32)], axis=1)

    def south(v):
        return jnp.concatenate([jnp.zeros((16, 1, 128), F32), v[:, :-1]], axis=1)

    def above(v):
        edge = jnp.where(group < 3, pltpu.roll(v[0:1], 96, 2), 0.0)
        return jnp.concatenate([v[1:], edge], axis=0)

    def below(v):
        edge = jnp.where(group > 0, pltpu.roll(v[15:16], 32, 2), 0.0)
        return jnp.concatenate([edge, v[:-1]], axis=0)

    total_scalar = sums_ref[0, 8]
    total = jnp.full((1, 24, 128), total_scalar, F32)
    theta = total + 6.0
    sigma = theta / 6.0
    kappa = known(1)

    def face(a, b):
        summed = a + b
        positive = summed > 0.0
        return jnp.where(positive, 2.0 * a * b / jnp.where(positive, summed, 1.0), 0.0)

    face_e = face(kappa, east(kappa))
    face_n = face(kappa, north(kappa))
    face_u = face(kappa, above(kappa))
    face_w = west(face_e)
    face_s = south(face_n)
    face_d = below(face_u)

    def operator(v):
        out = face_e * (east(v) - v) + face_w * (west(v) - v)
        out = out + face_n * (north(v) - v) + face_s * (south(v) - v)
        out = out + face_u * (above(v) - v) + face_d * (below(v) - v)
        return total * v - out

    def chebyshev(rhs):
        rho = 1.0 / sigma
        residual = rhs
        direction = rhs / theta
        correction = direction
        for _ in range(SWEEPS - 1):
            residual = residual - operator(direction)
            rho_next = 1.0 / (2.0 * sigma - rho)
            direction = rho_next * rho * direction + 2.0 * rho_next / 6.0 * residual
            rho = rho_next
            correction = correction + direction
        return correction

    temp = known(0)
    moved = (temp, west(temp), east(temp), south(temp), north(temp), below(temp), above(temp))
    gain = [sums_ref[k, 7] for k in range(4)]
    rhs = 0.5 * (
        gain[1] * (moved[2] - moved[1]) + gain[2] * (moved[4] - moved[3]) + gain[3] * (moved[6] - moved[5])
    )
    rhs = -(field(1) + rhs)
    once = (field(0) + gain[0] * temp) / total + chebyshev(rhs)

    def second(k, part):
        value = part + gain[k] * once
        for s in range(7):
            value = value + sums_ref[k, s] * moved[s]
        return value

    flux = [second(k, field(k + 1)) * inside for k in (1, 2, 3)]
    own = own_ref[5]
    energy = second(0, jnp.concatenate([own, own, own], axis=1))
    rhs = -0.5 * (
        (east(flux[0]) - west(flux[0])) + (north(flux[1]) - south(flux[1])) + (above(flux[2]) - below(flux[2]))
    )
    twice = energy / total + chebyshev(rhs)
    temp_ref[...] = twice[:, 8:16]
    for n in range(3):
        flux_ref[n] = flux[n][:, 8:16]


def solved(idx, sums, own, south, north, known):
    vmem = pl.BlockSpec(memory_space=pltpu.VMEM)
    smem = pl.BlockSpec(memory_space=pltpu.SMEM)
    return pl.pallas_call(
        solve_kernel,
        in_specs=[smem, smem] + [vmem] * 4,
        out_specs=[vmem, vmem],
        out_shape=[
            jax.ShapeDtypeStruct((16, 8, 128), F32),
            jax.ShapeDtypeStruct((3, 16, 8, 128), F32),
        ],
        compiler_params=pltpu.CompilerParams(vmem_limit_bytes=48 << 20),
        name="solve",
    )(idx, sums, own, south, north, known)


LINE = ("zy", "core")


def both_ways(value, axis, count):
    ahead = [(i, i + 1) for i in range(count - 1)]
    behind = [(i + 1, i) for i in range(count - 1)]
    if isinstance(value, tuple):
        tail, head = value
    else:
        tail = head = value
    return lax.ppermute(tail, axis, ahead), lax.ppermute(head, axis, behind)


def per_device(
    excess_phonon_enthalpy,
    thermal_offset,
    state_specific_warmth_scaled,
    scattering_lifetimes,
    state_polarization_label,
    state_orientation_label,
    polarization_propagation_rate,
    thermal_conductance_bulk,
    substance_label,
):
    space = lax.axis_index("space")
    core = lax.axis_index("core")
    line = lax.axis_index("zy") * 2 + core
    kappa = thermal_conductance_bulk * jnp.where(substance_label == 1, 0.1, 1.0)
    known = jnp.stack([thermal_offset, kappa])
    west, east = both_ways((known[:, 8:], known[:, :8]), "space", 8)
    known = jnp.concatenate([west, known, east], axis=1)
    known = known.reshape(2, 32, 8, 4, 16).transpose(0, 4, 2, 3, 1).reshape(2, 16, 8, 128)

    table = jnp.stack(
        [
            state_polarization_label.astype(F32),
            state_orientation_label.astype(F32),
            state_specific_warmth_scaled,
            scattering_lifetimes,
        ]
    )
    keep, send = moments(
        jnp.stack([space, core]).astype(jnp.int32),
        polarization_propagation_rate,
        table,
        excess_phonon_enthalpy,
    )
    received = lax.ppermute(send, "core", [(0, 1), (1, 0)])
    paired = (keep.astype(F32) + received.astype(F32)).astype(BF16)
    got = lax.all_to_all(paired, "zy", 0, 0, tiled=True)
    pieces, sums = at_owner(got)
    pieces = lax.all_to_all(pieces, "space", 0, 0, tiled=True)
    own, halo = merged(pieces, known)
    south, north = both_ways(halo, LINE, 16)
    temp, flux = solved(jnp.stack([space, line]).astype(jnp.int32), sums, own, south, north, known)

    def unpacked(value):
        lead = value.shape[:-3]
        n = len(lead)
        value = value.reshape(lead + (16, 8, 4, 32))[..., 8:24]
        order = tuple(range(n)) + tuple(n + d for d in (3, 1, 2, 0))
        return value.transpose(order).reshape(lead + (16, 8, 64))

    return unpacked(temp), unpacked(flux)


def solution(mesh):
    parts = Mesh(mesh.devices.reshape(8, 8, 2), ("space", "zy", "core"))
    modes = P(LINE)
    block = P("space", LINE, None)
    return jax.shard_map(
        per_device,
        mesh=parts,
        in_specs=(P(LINE, "space", None, None), block, modes, modes, modes, modes, P(), block, block),
        out_specs=(block, P(None, "space", LINE, None)),
        check_vma=False,
    )
```

time: 627 us -> 112 us (0.18)
  the two profiles are of different devices: /device:TPU:70 before, /device:TPU:57 now
where the time goes in v1:
time: 112 us
  Pallas kernels  30.8 us (28%)
  waiting for transfers between devices  24.4 us (22%)
  blocking collectives  22.9 us (20%)
  starting transfers between devices  21.3 us (19%)
  local copies, waits for them, and re-layouts  9.34 us (8%)
  other arithmetic  2.15 us (2%)
    pallas_call x1, Pallas kernels, moments(): pl.pallas_call(moments_kernel, grid=(SLAB,), in_specs=[pl.BlockSpec(memor...  23.2 us
    all_to_all x1, blocking collectives, per_device(): got = lax.all_to_all(paired, 'zy', 0, 0, tiled=True)  22.9 us
    ppermute x4, waiting for transfers between devices, both_ways(): return (lax.ppermute(tail, axis, ahead), lax.ppermute(head, axis, behind))  21.9 us
    ppermute x4, starting transfers between devices, both_ways(): return (lax.ppermute(tail, axis, ahead), lax.ppermute(head, axis, behind))  15.5 us
    all_to_all x1, starting transfers between devices, per_device(): pieces = lax.all_to_all(pieces, 'space', 0, 0, tiled=True)  5.2 us
    unnamed x16, local copies, waits for them, and re-layouts  3.33 us
    pallas_call x1, Pallas kernels, solved(): pl.pallas_call(solve_kernel, in_specs=[smem, smem] + [vmem] * 4, out_spec...  2.71 us
    pallas_call x1, Pallas kernels, at_owner(): pl.pallas_call(owner_kernel, out_shape=[jax.ShapeDtypeStruct((8, 216, 128...  2.63 us
  transfers between devices with their start and end apart: 6, of which 5 were waited for; matrix products, arithmetic and copies ran while one was open for 2% of the time, Pallas kernels for 0%

profile of v1, /device:TPU:57, one launch (start us, length us, event | category | flops | bytes accessed | tf_op | source)
XLA Modules:
  0.0 111.7 jit_solution(13742118352568316450)
XLA Ops:
  0.6 0.1 pad_add_fusion.1.idx_ref
  0.7 0.7 convert_bitcast_fusion
  1.4 0.7 pad_maximum_fusion.2.par_ref
  2.1 0.0 copy-start.3
  2.1 0.7 copy-done.3
  2.7 23.2 %moments.1 = (f32[8,592,128]{2,1,0:T(8,128)S(1)}, bf16[8,592,128]{2,1,0:T(8,128)(2,1)S(1)}) custom-call(s32[2]{0:T(128)S(1)} %pad_add_fusion.1.idx_ref, f32[6]{0:T(128)S(1)} %copy-done.3, f32[4,48]{1,0:T(4,128)S(1)} %pad_maximum_fusion.2.par_ref, bf16[48,8,128,128]{3,2,1,0:T(8,128)(2,1)} %e_ref.1), custom_call_target="tpu_custom_call" | custom-call | flops 20000000000 | bytes 16000000 | tf_op jit(solution)/shard_map/moments/pallas_call | solution.py:272
  26.0 0.6 collective-permute-start
  26.6 2.5 %collective-permute-done = bf16[8,592,128]{2,1,0:T(8,128)(2,1)S(1)} collective-permute-done((bf16[8,592,128]{2,1,0:T(8,128)(2,1)S(1)}, bf16[8,592,128]{2,1,0:T(8,128)(2,1)S(1)}, u32[]{:S(2)}, u32[]{:S(2)}) %collective-permute-start) | collective-permute-done | bytes 1212448 | tf_op jit(solution)/shard_map/ppermute | solution.py:548
  29.1 0.3 add_convert_fusion
  29.4 22.9 %all_to_all.10.got_ref = bf16[8,592,128]{2,1,0:T(8,128)(2,1)} all-to-all(bf16[8,592,128]{2,1,0:T(8,128)(2,1)S(1)} %add_convert_fusion), channel_id=1, replica_groups=mesh['space'=8,'zy'=8,'core'=2] {'zy'}, dimensions={0} | all-to-all | bytes 2424832 | tf_op jit(solution)/shard_map/all_to_all | solution.py:550
  52.3 0.0 copy-start.6
  52.3 0.0 copy-start.7
  52.3 2.6 %owner.1 = (bf16[8,216,128]{2,1,0:T(8,128)(2,1)}, f32[8,128]{1,0:T(8,128)}) custom-call(bf16[8,592,128]{2,1,0:T(8,128)(2,1)} %all_to_all.10.got_ref), custom_call_target="tpu_custom_call" | custom-call | tf_op jit(solution)/shard_map/owner/pallas_call | solution.py:331
  54.9 5.2 %all-to-all-start.1 = ((bf16[8,216,128]{2,1,0:T(8,128)(2,1)}), bf16[8,216,128]{2,1,0:T(8,128)(2,1)S(1)}, u32[]{:S(2)}, u32[]{:S(2)}) async-start(bf16[8,216,128]{2,1,0:T(8,128)(2,1)} %get-tuple-element.13), calls=%async_computation.1 | async-start | bytes 884736 | tf_op jit(solution)/shard_map/all_to_all | solution.py:552
  60.1 0.0 copy-done.6
  60.1 0.0 copy-done.7
  60.1 0.0 copy-done.5
  60.2 0.2 copy.21
  60.4 4.3 %collective-permute-start.2 = (f32[2,8,8,64]{1,3,2,0:T(8,128)S(1)}, f32[2,8,8,64]{1,3,2,0:T(8,128)S(1)}, u32[]{:S(2)}, u32[]{:S(2)}) collective-permute-start(f32[2,8,8,64]{1,3,2,0:T(8,128)S(1)} %copy.21), channel_id=1, source_target_pairs={{16,0},{32,16},{48,32},{64,48},{80,64},{96,80},{112,96},{17,1},{33... | collective-permute-start | bytes 98312 | tf_op jit(solution)/shard_map/ppermute | solution.py:511
  64.7 0.2 copy.20
  64.9 1.9 %collective-permute-start.1 = (f32[2,8,8,64]{1,3,2,0:T(8,128)S(1)}, f32[2,8,8,64]{1,3,2,0:T(8,128)S(1)}, u32[]{:S(2)}, u32[]{:S(2)}) collective-permute-start(f32[2,8,8,64]{1,3,2,0:T(8,128)S(1)} %copy.20), channel_id=1, source_target_pairs={{0,16},{16,32},{32,48},{48,64},{64,80},{80,96},{96,112},{1,17},{17... | collective-permute-start | bytes 98312 | tf_op jit(solution)/shard_map/ppermute | solution.py:511
  66.9 0.2 copy.22
  67.1 9.2 %collective-permute-done.2 = f32[2,8,8,64]{1,3,2,0:T(8,128)S(1)} collective-permute-done((f32[2,8,8,64]{1,3,2,0:T(8,128)S(1)}, f32[2,8,8,64]{1,3,2,0:T(8,128)S(1)}, u32[]{:S(2)}, u32[]{:S(2)}) %collective-permute-start.2) | collective-permute-done | bytes 32800 | tf_op jit(solution)/shard_map/ppermute | solution.py:511
  76.2 3.6 %collective-permute-done.1 = f32[2,8,8,64]{1,3,2,0:T(8,128)S(1)} collective-permute-done((f32[2,8,8,64]{1,3,2,0:T(8,128)S(1)}, f32[2,8,8,64]{1,3,2,0:T(8,128)S(1)}, u32[]{:S(2)}, u32[]{:S(2)}) %collective-permute-start.1) | collective-permute-done | bytes 32800 | tf_op jit(solution)/shard_map/ppermute | solution.py:511
  79.8 0.3 pad_maximum_fusion
  80.2 0.0 copy-start.2
  80.2 0.2 copy.23
  80.4 0.9 reshape.23.known_ref
  81.3 0.0 all-to-all-done.1.got_ref
  81.3 0.8 copy-done.4
  82.1 2.2 %merge.1 = (f32[6,16,8,128]{3,2,1,0:T(8,128)}, bf16[896,128]{1,0:T(8,128)(2,1)}) custom-call(bf16[8,216,128]{2,1,0:T(8,128)(2,1)} %copy-done.4, f32[2,16,8,128]{3,2,1,0:T(8,128)} %reshape.23.known_ref), custom_call_target="tpu_custom_call" | custom-call | tf_op jit(solution)/shard_map/merge/pallas_call | solution.py:372
  84.3 7.4 %collective-permute-start.3 = (bf16[896,128]{1,0:T(8,128)(2,1)}, bf16[896,128]{1,0:T(8,128)(2,1)S(1)}, u32[]{:S(2)}, u32[]{:S(2)}) collective-permute-start(bf16[896,128]{1,0:T(8,128)(2,1)} %get-tuple-element.15), channel_id=1, source_target_pairs={{0,1},{1,2},{2,3},{3,4},{4,5},{5,6},{6,7},{7,8},{8,9},{9,10},{10,1... | collective-permute-start | bytes 688136 | tf_op jit(solution)/shard_map/ppermute | solution.py:511
  91.7 1.9 %collective-permute-start.4 = (bf16[896,128]{1,0:T(8,128)(2,1)}, bf16[896,128]{1,0:T(8,128)(2,1)S(1)}, u32[]{:S(2)}, u32[]{:S(2)}) collective-permute-start(bf16[896,128]{1,0:T(8,128)(2,1)} %get-tuple-element.15), channel_id=1, source_target_pairs={{1,0},{2,1},{3,2},{4,3},{5,4},{6,5},{7,6},{8,7},{9,8},{10,9},{11,1... | collective-permute-start | bytes 688136 | tf_op jit(solution)/shard_map/ppermute | solution.py:511
  93.6 0.1 pad_add_fusion.idx_ref
  93.7 1.2 %collective-permute-done.3.south_ref = bf16[896,128]{1,0:T(8,128)(2,1)S(1)} collective-permute-done((bf16[896,128]{1,0:T(8,128)(2,1)}, bf16[896,128]{1,0:T(8,128)(2,1)S(1)}, u32[]{:S(2)}, u32[]{:S(2)}) %collective-permute-start.3) | collective-permute-done | bytes 229408 | tf_op jit(solution)/shard_map/ppermute | solution.py:511
  94.9 7.9 %collective-permute-done.4.north_ref = bf16[896,128]{1,0:T(8,128)(2,1)S(1)} collective-permute-done((bf16[896,128]{1,0:T(8,128)(2,1)}, bf16[896,128]{1,0:T(8,128)(2,1)S(1)}, u32[]{:S(2)}, u32[]{:S(2)}) %collective-permute-start.4) | collective-permute-done | bytes 229408 | tf_op jit(solution)/shard_map/ppermute | solution.py:511
  102.8 0.0 copy-done.2
  102.8 0.9 copy-done
  103.7 1.0 copy-done.1
  104.7 2.7 %solve.1 = (f32[16,8,128]{2,1,0:T(8,128)S(1)}, f32[3,16,8,128]{3,2,1,0:T(8,128)S(1)}) custom-call(s32[2]{0:T(128)S(1)} %pad_add_fusion.idx_ref, f32[8,128]{1,0:T(8,128)S(1)} %copy-done.2, f32[6,16,8,128]{3,2,1,0:T(8,128)S(1)} %copy-done.1, bf16[896,128]{1,0:T(8,128)(2,1)S(1)} %collective-permute-done.3.south_ref, ...), custom_call_target="tpu_custom_call" | custom-call | tf_op jit(solution)/shard_map/solve/pallas_call | solution.py:488
  107.4 0.2 reshape.24
  107.6 0.2 slice_bitcast_fusion.1
  107.8 0.3 copy.24
  108.1 0.8 reshape.25
  108.9 0.3 reshape.26
  109.3 0.5 slice_bitcast_fusion
  109.8 0.9 copy.25
  110.7 1.0 reshape.27
  (7 shorter events, 0.0 us)
Async XLA Ops:
  2.1 0.7 copy-start.3
  26.0 3.1 %collective-permute-start = (bf16[8,592,128]{2,1,0:T(8,128)(2,1)S(1)}, bf16[8,592,128]{2,1,0:T(8,128)(2,1)S(1)}, u32[]{:S(2)}, u32[]{:S(2)}) collective-permute-start(bf16[8,592,128]{2,1,0:T(8,128)(2,1)S(1)} %get-tuple-element.11), channel_id=1, source_target_pairs={{0,1},{1,0},{2,3},{3,2},{4,5},{5,4},{6,7},{7,6},{8,9},{9,8},{10,11... | collective-permute-start | bytes 3637256 | tf_op jit(solution)/shard_map/ppermute | solution.py:548
  52.3 7.8 %copy-start.6 = (f32[16,8,64]{2,1,0:T(8,128)S(1)}, f32[16,8,64]{2,1,0:T(8,128)}, u32[]{:S(2)}) copy-start(f32[16,8,64]{2,1,0:T(8,128)} %param.16) | copy-start | bytes 98308
  52.3 7.8 %copy-start.7 = (s32[16,8,64]{2,1,0:T(8,128)S(1)}, s32[16,8,64]{2,1,0:T(8,128)}, u32[]{:S(2)}) copy-start(s32[16,8,64]{2,1,0:T(8,128)} %param.17) | copy-start | bytes 98308
  52.3 7.9 %copy-start.5 = (f32[16,8,64]{2,1,0:T(8,128)S(1)}, f32[16,8,64]{2,1,0:T(8,128)}, u32[]{:S(2)}) copy-start(f32[16,8,64]{2,1,0:T(8,128)} %param.10) | copy-start | bytes 98308
  54.9 26.4 %all-to-all-start.1 = ((bf16[8,216,128]{2,1,0:T(8,128)(2,1)}), bf16[8,216,128]{2,1,0:T(8,128)(2,1)S(1)}, u32[]{:S(2)}, u32[]{:S(2)}) async-start(bf16[8,216,128]{2,1,0:T(8,128)(2,1)} %get-tuple-element.13), calls=%async_computation.1 | async-start | bytes 884736 | tf_op jit(solution)/shard_map/all_to_all | solution.py:552
  60.4 15.9 %collective-permute-start.2 = (f32[2,8,8,64]{1,3,2,0:T(8,128)S(1)}, f32[2,8,8,64]{1,3,2,0:T(8,128)S(1)}, u32[]{:S(2)}, u32[]{:S(2)}) collective-permute-start(f32[2,8,8,64]{1,3,2,0:T(8,128)S(1)} %copy.21), channel_id=1, source_target_pairs={{16,0},{32,16},{48,32},{64,48},{80,64},{96,80},{112,96},{17,1},{33... | collective-permute-start | bytes 98312 | tf_op jit(solution)/shard_map/ppermute | solution.py:511
  64.9 14.9 %collective-permute-start.1 = (f32[2,8,8,64]{1,3,2,0:T(8,128)S(1)}, f32[2,8,8,64]{1,3,2,0:T(8,128)S(1)}, u32[]{:S(2)}, u32[]{:S(2)}) collective-permute-start(f32[2,8,8,64]{1,3,2,0:T(8,128)S(1)} %copy.20), channel_id=1, source_target_pairs={{0,16},{16,32},{32,48},{48,64},{64,80},{80,96},{96,112},{1,17},{17... | collective-permute-start | bytes 98312 | tf_op jit(solution)/shard_map/ppermute | solution.py:511
  80.2 22.7 %copy-start.2 = (f32[8,128]{1,0:T(8,128)S(1)}, f32[8,128]{1,0:T(8,128)}, u32[]{:S(2)}) copy-start(f32[8,128]{1,0:T(8,128)} %get-tuple-element.12.sums_ref) | copy-start | bytes 12292
  81.3 0.8 copy-start.4
  84.3 10.6 %collective-permute-start.3 = (bf16[896,128]{1,0:T(8,128)(2,1)}, bf16[896,128]{1,0:T(8,128)(2,1)S(1)}, u32[]{:S(2)}, u32[]{:S(2)}) collective-permute-start(bf16[896,128]{1,0:T(8,128)(2,1)} %get-tuple-element.15), channel_id=1, source_target_pairs={{0,1},{1,2},{2,3},{3,4},{4,5},{5,6},{6,7},{7,8},{8,9},{9,10},{10,1... | collective-permute-start | bytes 688136 | tf_op jit(solution)/shard_map/ppermute | solution.py:511
  91.7 11.2 %collective-permute-start.4 = (bf16[896,128]{1,0:T(8,128)(2,1)}, bf16[896,128]{1,0:T(8,128)(2,1)S(1)}, u32[]{:S(2)}, u32[]{:S(2)}) collective-permute-start(bf16[896,128]{1,0:T(8,128)(2,1)} %get-tuple-element.15), channel_id=1, source_target_pairs={{1,0},{2,1},{3,2},{4,3},{5,4},{6,5},{7,6},{8,7},{9,8},{10,9},{11,1... | collective-permute-start | bytes 688136 | tf_op jit(solution)/shard_map/ppermute | solution.py:511
  102.8 0.9 copy-start
  103.7 1.0 copy-start.1

commit v2 on v1

--- a/solution.py
+++ b/solution.py
@@ -6,7 +6,6 @@
 from jax.experimental import pallas as pl
 from jax.experimental.pallas import tpu as pltpu
 from jax.sharding import Mesh, PartitionSpec as P
-
 
 SWEEPS = 4
 STEP = 0.25
@@ -15,12 +14,15 @@
 SLAB = 8
 NX = 128
 NY = 128
+NZ = 64
 WIN = 5 * LOCAL
 DEPTH = 256
 EXT = 12
 PITCH = 17
-ROWS = 6 * EXT * 8
-PIECE = ROWS + 16
+PACE = 9
+LAYERS = 6 * EXT
+DEPTHS = LAYERS // 8
+PIECE = DEPTHS * 8
 F32 = jnp.float32
 BF16 = jnp.bfloat16
 
@@ -135,20 +137,17 @@
     sums = jnp.zeros((8, 128), F32)
     for n, column in enumerate(columns):
         sums = jnp.where(lane == n, jnp.sum(column, axis=1, keepdims=True), sums)
+    row = lax.broadcasted_iota(jnp.int32, (8, 128), 0)
+    sums = jnp.where((row // 4) == core, sums, 0.0)
     high = sums.astype(BF16).astype(F32)
-    rest = sums - high
-    middle = rest.astype(BF16).astype(F32)
-    low = rest - middle
-    packed = high + pltpu.roll(middle, 16, 1) + pltpu.roll(low, 32, 1)
-    packed = jnp.where(core == 0, packed, pltpu.roll(packed, 64, 1))
-    return jnp.concatenate([packed, jnp.zeros((8, 128), F32)], axis=0).astype(BF16)
-
-
-def moments_kernel(idx_ref, prop_ref, par_ref, e_ref, keep_ref, send_ref, par5, coef, spread, turned, acc):
+    return high, pltpu.roll(sums - high, 48, 1)
+
+
+def moments_kernel(idx_ref, prop_ref, par_ref, e_ref, keep_ref, send_ref, par5, coef, spread, turned, acc, drift):
     z = pl.program_id(0)
     space = idx_ref[0]
     core = idx_ref[1]
-    LAYER = NX * 8
+    LAYER = NX * PACE
 
     @pl.when(z == 0)
     def _():
@@ -162,14 +161,14 @@
 
         acc[13 * LAYER : 14 * LAYER, :] = jnp.zeros((LAYER, 128), F32)
 
-    @pl.loop(0, NX // 16)
-    def _(c):
-        x0 = pl.multiple_of(c * 16, 16)
+    def turn(c):
         for m in range(LOCAL):
-            spread[m * PITCH : m * PITCH + 16, :] = e_ref[m, 0, pl.ds(x0, 16), :].astype(F32)
+            at = (c * LOCAL + m) * PITCH
+            spread[at : at + 16, :] = e_ref[m, 0, 16 * c : 16 * c + 16, :].astype(F32)
         for xx in range(16):
-            rows = spread[pl.ds(xx, LOCAL, stride=PITCH), :].astype(BF16)
-            turned[pl.ds(pl.multiple_of((x0 + (xx + 2)) * LOCAL, 16), LOCAL), :] = rows
+            rows = spread[pl.ds(c * LOCAL * PITCH + xx, LOCAL, stride=PITCH), :].astype(BF16)
+            at = (16 * c + xx + 2) * LOCAL
+            turned[at : at + LOCAL, :] = rows
 
     lane = lane_iota((8, 128))
 
@@ -192,14 +191,19 @@
                         if n == 0:
                             part = part + out[8 * NS :, 128 * half : 128 * half + 128]
                         total = part if total is None else total + part
-                    at = pl.multiple_of((z + 3 + sz) * LAYER + (x + half) * 8, 8)
+                    at = (z + 3 + sz) * LAYER + (x + half) * PACE
                     if sz == 2:
                         acc[pl.ds(at, 8), :] = total
                     else:
                         acc[pl.ds(at, 8), :] += total
 
-    for x in range(0, NX, 2):
-        one_pair(x)
+    CHUNKS = NX // 16
+    turn(0)
+    for c in range(CHUNKS):
+        if c + 1 < CHUNKS:
+            turn(c + 1)
+        for x in range(16 * c, 16 * c + 16, 2):
+            one_pair(x)
 
     @pl.when(z == SLAB - 1)
     def _():
@@ -211,14 +215,11 @@
         def _():
             acc[11 * LAYER : 13 * LAYER, :] = jnp.zeros((2 * LAYER, 128), F32)
 
-        def give(ref, block, at, tile):
-            ref[block, pl.ds(at, 16), :] = tile.astype(ref.dtype)
-
         row = lax.broadcasted_iota(jnp.int32, (NX, 128), 0)
         col = lane_iota((NX, 128))
 
         def layer(zo, field, shift=0):
-            return acc[pl.ds((zo + 1) * LAYER + field + 8 * shift, NX, stride=8), :]
+            return acc[pl.ds((zo + 1) * LAYER + field + PACE * shift, NX, stride=PACE), :]
 
         def divergence(zo):
             east = jnp.where(row < NX - 1, layer(zo, 1, 1), 0.0)
@@ -230,45 +231,33 @@
             down = layer(zo - 1, 3)
             return 0.5 * ((east - west) + (north - south) + (up - down))
 
-        sources = (
-            lambda zo: layer(zo, 0),
-            divergence,
-            lambda zo: layer(zo, 5),
-            lambda zo: layer(zo, 6),
-            lambda zo: layer(zo, 7),
-            lambda zo: layer(zo, 4),
-        )
-        for f, source in enumerate(sources):
-
-            @pl.loop(0, EXT // 2)
-            def _(pair):
-                zo = pair * 2
-                even = source(zo).T
-                odd = source(zo + 1).T
-                at = pl.multiple_of((f * EXT + zo) * 8, 16)
-                tiles = [
-                    jnp.concatenate([even[8 * j : 8 * j + 8], odd[8 * j : 8 * j + 8]], axis=0)
-                    for j in range(16)
-                ]
-
-                @pl.when(core == 0)
-                def _():
-                    for j in range(16):
-                        give(send_ref if j % 2 else keep_ref, j // 2, at, tiles[j])
-
-                @pl.when(core == 1)
-                def _():
-                    for j in range(16):
-                        give(keep_ref if j % 2 else send_ref, j // 2, at, tiles[j])
-
-        sums = mode_sums(par_ref, prop_ref, core)
-        for p in range(8):
-            keep_ref[p, ROWS:PIECE, :] = sums.astype(F32)
-            send_ref[p, ROWS:PIECE, :] = sums
+        for zo in range(EXT):
+            drift[zo * NX : zo * NX + NX, :] = divergence(zo)
+        rows = (0, None, 5, 6, 7, 4)
+        extras = mode_sums(par_ref, prop_ref, core)
+
+        def strip(depth, i):
+            f, zo = divmod(depth, EXT)
+            if rows[f] is None:
+                return drift[zo * NX + 16 * i : zo * NX + 16 * i + 16, :]
+            return acc[pl.ds((zo + 1) * LAYER + rows[f] + 16 * i * PACE, 16, stride=PACE), :]
+
+        for d in range(DEPTHS):
+            for i in range(8):
+                tile = jnp.concatenate([strip(8 * d + low, i) for low in range(8)], axis=0).T
+                for p in range(8):
+                    first, second = tile[16 * p : 16 * p + 8], tile[16 * p + 8 : 16 * p + 16]
+                    kept = jnp.where(core == 0, first, second)
+                    sent = jnp.where(core == 0, second, first)
+                    if d < 2:
+                        kept = kept + extras[d]
+                        sent = sent + extras[d]
+                    keep_ref[8 * i + p, 8 * d : 8 * d + 8, :] = kept
+                    send_ref[8 * i + p, 8 * d : 8 * d + 8, :] = sent.astype(BF16)
 
 
 def moments(idx, prop, par, state):
-    whole = pl.BlockSpec((8, PIECE, 128), lambda z: (0, 0, 0))
+    whole = pl.BlockSpec((64, PIECE, 128), lambda z: (0, 0, 0))
     return pl.pallas_call(
         moments_kernel,
         grid=(SLAB,),
@@ -279,13 +268,14 @@
             pl.BlockSpec((LOCAL, 1, NX, NY), lambda z: (0, z, 0, 0)),
         ],
         out_specs=[whole, whole],
-        out_shape=[jax.ShapeDtypeStruct((8, PIECE, 128), t) for t in (F32, BF16)],
+        out_shape=[jax.ShapeDtypeStruct((64, PIECE, 128), t) for t in (F32, BF16)],
         scratch_shapes=[
             pltpu.VMEM((8, DEPTH), F32),
             pltpu.VMEM((NS * 8 + 8, DEPTH), BF16),
-            pltpu.VMEM((LOCAL * PITCH + 8, 128), F32),
+            pltpu.VMEM((8 * LOCAL * PITCH + 8, 128), F32),
             pltpu.VMEM(((NX + 4) * LOCAL + 16, 128), BF16),
-            pltpu.VMEM((14 * NX * 8, 128), F32),
+            pltpu.VMEM((14 * NX * PACE, 128), F32),
+            pltpu.VMEM((EXT * NX, 128), F32),
         ],
         compiler_params=pltpu.CompilerParams(vmem_limit_bytes=48 << 20),
         cost_estimate=pl.CostEstimate(flops=20_000_000_000, bytes_accessed=16_000_000, transcendentals=0),
@@ -293,93 +283,121 @@
     )(idx, prop, par, state)
 
 
-def owner_kernel(got_ref, out_ref, sums_ref):
+def gather_kernel(got_ref, temp_ref, bulk_ref, label_ref, own_ref, known_ref, edge_ref, sums_ref, total):
     lane = lane_iota((8, 128))
-    part = lane % 32
+    group = lane // 32
+    inner = (lane % 32 >= 8) & (lane % 32 < 24)
+    for s in range(8):
+        for d in range(DEPTHS):
+            value = got_ref[8 * s, 8 * d : 8 * d + 8, :].astype(F32)
+            for q in range(1, 8):
+                value = value + got_ref[8 * s + q, 8 * d : 8 * d + 8, :].astype(F32)
+            total[s * DEPTHS + d] = value
+
+    sums = total[0] + pltpu.roll(total[1], 80, 1)
+    sums_ref[...] = sums + pltpu.roll(sums, 4, 0)
+
+    def layer(s, f, zo, quarter):
+        depth = f * EXT + zo
+        turn = (32 * quarter + 8 - 16 * (depth % 8)) % 128
+        value = total[s * DEPTHS + depth // 8]
+        return pltpu.roll(value, turn, 1) if turn else value
+
     for f in range(6):
-        for high in range(EXT // 4):
-            base = (f * EXT + high * 4) * 8
-            layers = got_ref[0, base : base + 32, :].astype(F32)
-            for m in range(1, 8):
-                layers = layers + got_ref[m, base : base + 32, :].astype(F32)
-            tiles = []
-            for i in range(8):
-                value = None
-                for low in range(4):
-                    rolled = pltpu.roll(layers[8 * low : 8 * low + 8], (32 * low - 16 * i + 8) % 128, 1)
-                    value = rolled if low == 0 else jnp.where(lane >= 32 * low, rolled, value)
-                if i == 0:
-                    value = jnp.where(part >= 8, value, 0.0)
-                if i == 7:
-                    value = jnp.where(part < 24, value, 0.0)
-                tiles.append(value)
-            at = (f * 3 + high) * 8
-            for i in range(8):
-                out_ref[i, at : at + 8, :] = tiles[i].astype(BF16)
-                if f in (2, 3, 4):
-                    low = tiles[i] - tiles[i].astype(BF16).astype(F32)
-                    out_ref[i, at + 96 : at + 104, :] = low.astype(BF16)
-    total = got_ref[0, ROWS:PIECE, :].astype(F32)
-    for m in range(1, 8):
-        total = total + got_ref[m, ROWS:PIECE, :].astype(F32)
-    total = total[0:8]
-    total = total + pltpu.roll(total, 64, 1)
-    sums_ref[...] = total + pltpu.roll(total, 112, 1) + pltpu.roll(total, 96, 1)
-
-
-def at_owner(got):
-    return pl.pallas_call(
-        owner_kernel,
-        out_shape=[
-            jax.ShapeDtypeStruct((8, 216, 128), BF16),
-            jax.ShapeDtypeStruct((8, 128), F32),
-        ],
-        name="owner",
-    )(got)
-
-
-def merge_kernel(got_ref, known_ref, own_ref, halo_ref):
-    group = lane_iota((8, 128)) // 32
-
-    def layer(s, f, zo, quarter):
-        at = (f * 3 + zo // 4) * 8
-        value = got_ref[s, at : at + 8, :].astype(F32)
-        if f in (2, 3, 4):
-            value = value + got_ref[s, at + 96 : at + 104, :].astype(F32)
-        turn = (32 * (quarter - zo % 4)) % 128
-        return pltpu.roll(value, turn, 1) if turn else value
-
-    for f in range(6):
+        reach = 1 if f == 0 else 2
         for zz in range(16):
             value = None
             for quarter in range(4):
                 z = quarter * 16 + zz
                 s = z // 8
                 part = layer(s, f, z % 8 + 2, quarter)
-                if z % 8 < 2 and s > 0:
+                if z % 8 < reach and s > 0:
                     part = part + layer(s - 1, f, z % 8 + 10, quarter)
-                if z % 8 > 5 and s < 7:
+                if z % 8 > 7 - reach and s < 7:
                     part = part + layer(s + 1, f, z % 8 - 6, quarter)
                 value = part if quarter == 0 else jnp.where(group >= quarter, part, value)
             own_ref[f, zz] = value
-            if f < 5:
-                halo_ref[(f * 16 + zz) * 8 : (f * 16 + zz) * 8 + 8, :] = value.astype(BF16)
-    for n in range(2):
-        halo_ref[640 + 128 * n : 768 + 128 * n, :] = known_ref[n].reshape(128, 128).astype(BF16)
-
-
-def merged(got, known):
+
+    wide_group = lane_iota((16, 128)) // 32
+
+    def block_of(n, read):
+        cells = jnp.concatenate([read(pl.ds(y, 16, stride=8)) for y in range(8)], axis=0).T
+        for y in range(8):
+            value = None
+            for quarter in range(4):
+                turn = (32 * quarter + 8 - 16 * y) % 128
+                part = cells[16 * quarter : 16 * quarter + 16]
+                part = pltpu.roll(part, turn, 1) if turn else part
+                value = part if quarter == 0 else jnp.where(wide_group >= quarter, part, value)
+            known_ref[n, pl.ds(y, 16, stride=8), :] = value
+
+    block_of(0, lambda rows: temp_ref[rows, :])
+    block_of(1, lambda rows: bulk_ref[rows, :] * jnp.where(label_ref[rows, :] == 1, 0.1, 1.0))
+
+    for n in range(7):
+
+        def cells(zz):
+            if n < 5:
+                return own_ref[n, zz]
+            return known_ref[n - 5, 8 * zz : 8 * zz + 8, :]
+
+        for h in range(8):
+            packed = jnp.where(inner, cells(2 * h), pltpu.roll(cells(2 * h + 1), 16, 1))
+            edge_ref[(n * 8 + h) * 8 : (n * 8 + h) * 8 + 8, :] = packed.astype(BF16)
+
+
+def gathered(got, temp, bulk, label):
+    flat = [value.reshape(128, NZ) for value in (temp, bulk, label)]
     return pl.pallas_call(
-        merge_kernel,
+        gather_kernel,
         out_shape=[
             jax.ShapeDtypeStruct((6, 16, 8, 128), F32),
-            jax.ShapeDtypeStruct((7 * 16 * 8, 128), BF16),
+            jax.ShapeDtypeStruct((2, 128, 128), F32),
+            jax.ShapeDtypeStruct((7 * 64, 128), BF16),
+            jax.ShapeDtypeStruct((8, 128), F32),
         ],
-        name="merge",
-    )(got, known)
-
-
-def solve_kernel(idx_ref, sums_ref, own_ref, south_ref, north_ref, known_ref, temp_ref, flux_ref):
+        scratch_shapes=[pltpu.VMEM((8 * DEPTHS, 8, 128), F32)],
+        name="gather",
+    )(got, *flat)
+
+
+def widen_kernel(own_ref, known_ref, west_ref, east_ref, wide_ref, halo_ref):
+    part = lane_iota((8, 128)) % 32
+    for n in range(7):
+        for zz in range(16):
+            at = (n * 8 + zz // 2) * 8
+            west = pltpu.roll(west_ref[at : at + 8, :].astype(F32), 96 if zz % 2 else 112, 1)
+            east = east_ref[at : at + 8, :].astype(F32)
+            if zz % 2 == 0:
+                east = pltpu.roll(east, 16, 1)
+            own = own_ref[n, zz] if n < 5 else known_ref[n - 5, 8 * zz : 8 * zz + 8, :]
+            value = jnp.where(part < 8, west, jnp.where(part < 24, own, east))
+            wide_ref[n, zz] = value
+            halo_ref[(n * 16 + zz) * 8 : (n * 16 + zz) * 8 + 8, :] = value.astype(BF16)
+
+
+def widened(own, known, west, east):
+    return pl.pallas_call(
+        widen_kernel,
+        out_shape=[
+            jax.ShapeDtypeStruct((7, 16, 8, 128), F32),
+            jax.ShapeDtypeStruct((7 * 128, 128), BF16),
+        ],
+        name="widen",
+    )(own, known, west, east)
+
+
+def solve_kernel(
+    idx_ref, sums_ref, own_ref, south_hbm, north_hbm, wide_ref, temp_ref, flux_ref, halo, lines, sems
+):
+    copies = [
+        pltpu.make_async_copy(src, halo.at[n], sems.at[n]) for n, src in enumerate((south_hbm, north_hbm))
+    ]
+    for copy in copies:
+        copy.start()
+    for copy in copies:
+        copy.wait()
+    shape = (16, 24, 128)
     lane = lane_iota((1, 24, 128))
     x = lane % 32 + (idx_ref[0] * 16 - 8)
     y = lax.broadcasted_iota(jnp.int32, (1, 24, 128), 1) + (idx_ref[1] * 8 - 8)
@@ -388,15 +406,15 @@
 
     def wide(own, f):
         rows = slice(f * 128, f * 128 + 128)
-        south = south_ref[rows, :].astype(F32).reshape(16, 8, 128)
-        north = north_ref[rows, :].astype(F32).reshape(16, 8, 128)
+        south = halo[0, rows, :].astype(F32).reshape(16, 8, 128)
+        north = halo[1, rows, :].astype(F32).reshape(16, 8, 128)
         return jnp.concatenate([south, own, north], axis=1)
 
     def field(f):
-        return wide(own_ref[f], f)
+        return wide(wide_ref[f], f)
 
     def known(n):
-        return wide(known_ref[n], 5 + n)
+        return wide(wide_ref[5 + n], 5 + n)
 
     def east(v):
         return pltpu.roll(v, 127, 2)
@@ -447,7 +465,7 @@
         residual = rhs
         direction = rhs / theta
         correction = direction
-        for _ in range(SWEEPS - 1):
+        for sweep in range(SWEEPS - 1):
             residual = residual - operator(direction)
             rho_next = 1.0 / (2.0 * sigma - rho)
             direction = rho_next * rho * direction + 2.0 * rho_next / 6.0 * residual
@@ -477,25 +495,53 @@
         (east(flux[0]) - west(flux[0])) + (north(flux[1]) - south(flux[1])) + (above(flux[2]) - below(flux[2]))
     )
     twice = energy / total + chebyshev(rhs)
-    temp_ref[...] = twice[:, 8:16]
+    quarter = lane_iota((16, 128)) // 16
+
+    def write(n, value, store):
+        for zz in range(16):
+            lines[n, zz * PACE : zz * PACE + 8, :] = value[zz, 8:16]
+        rows = [lines[n, pl.ds(y, 16, stride=PACE), :] for y in range(8)]
+        turned = jnp.concatenate(rows, axis=0).T
+        for y in range(8):
+            out = None
+            for q in range(4):
+                part = turned[32 * q + 8 : 32 * q + 24]
+                move = (16 * (q - y)) % 128
+                part = pltpu.roll(part, move, 1) if move else part
+                out = part if q == 0 else jnp.where(quarter >= q, part, out)
+            store(y, out[:, :64])
+
+    def store_temp(y, out):
+        temp_ref[pl.ds(y, 16, stride=8), :] = out
+
+    write(0, twice, store_temp)
     for n in range(3):
-        flux_ref[n] = flux[n][:, 8:16]
-
-
-def solved(idx, sums, own, south, north, known):
+
+        def store_flux(y, out, n=n):
+            flux_ref[n, pl.ds(y, 16, stride=8), :] = out
+
+        write(n + 1, flux[n], store_flux)
+
+
+def solved(idx, sums, own, south, north, wide):
     vmem = pl.BlockSpec(memory_space=pltpu.VMEM)
     smem = pl.BlockSpec(memory_space=pltpu.SMEM)
     return pl.pallas_call(
         solve_kernel,
-        in_specs=[smem, smem] + [vmem] * 4,
+        in_specs=[smem, smem, vmem] + [pl.BlockSpec(memory_space=pl.ANY)] * 2 + [vmem],
         out_specs=[vmem, vmem],
         out_shape=[
-            jax.ShapeDtypeStruct((16, 8, 128), F32),
-            jax.ShapeDtypeStruct((3, 16, 8, 128), F32),
+            jax.ShapeDtypeStruct((128, 64), F32),
+            jax.ShapeDtypeStruct((3, 128, 64), F32),
+        ],
+        scratch_shapes=[
+            pltpu.VMEM((2, 7 * 128, 128), BF16),
+            pltpu.VMEM((4, 16 * PACE, 128), F32),
+            pltpu.SemaphoreType.DMA((2,)),
         ],
         compiler_params=pltpu.CompilerParams(vmem_limit_bytes=48 << 20),
         name="solve",
-    )(idx, sums, own, south, north, known)
+    )(idx, sums, own, south, north, wide)
 
 
 LINE = ("zy", "core")
@@ -504,11 +550,7 @@
 def both_ways(value, axis, count):
     ahead = [(i, i + 1) for i in range(count - 1)]
     behind = [(i + 1, i) for i in range(count - 1)]
-    if isinstance(value, tuple):
-        tail, head = value
-    else:
-        tail = head = value
-    return lax.ppermute(tail, axis, ahead), lax.ppermute(head, axis, behind)
+    return lax.ppermute(value, axis, ahead), lax.ppermute(value, axis, behind)
 
 
 def per_device(
@@ -525,12 +567,6 @@
     space = lax.axis_index("space")
     core = lax.axis_index("core")
     line = lax.axis_index("zy") * 2 + core
-    kappa = thermal_conductance_bulk * jnp.where(substance_label == 1, 0.1, 1.0)
-    known = jnp.stack([thermal_offset, kappa])
-    west, east = both_ways((known[:, 8:], known[:, :8]), "space", 8)
-    known = jnp.concatenate([west, known, east], axis=1)
-    known = known.reshape(2, 32, 8, 4, 16).transpose(0, 4, 2, 3, 1).reshape(2, 16, 8, 128)
-
     table = jnp.stack(
         [
             state_polarization_label.astype(F32),
@@ -546,22 +582,14 @@
         excess_phonon_enthalpy,
     )
     received = lax.ppermute(send, "core", [(0, 1), (1, 0)])
-    paired = (keep.astype(F32) + received.astype(F32)).astype(BF16)
-    got = lax.all_to_all(paired, "zy", 0, 0, tiled=True)
-    pieces, sums = at_owner(got)
-    pieces = lax.all_to_all(pieces, "space", 0, 0, tiled=True)
-    own, halo = merged(pieces, known)
+    paired = (keep + received.astype(F32)).astype(BF16)
+    got = lax.all_to_all(paired, ("space", "zy"), 0, 0, tiled=True)
+    own, known, edge, sums = gathered(got, thermal_offset, thermal_conductance_bulk, substance_label)
+    west, east = both_ways(edge, "space", 8)
+    wide, halo = widened(own, known, west, east)
     south, north = both_ways(halo, LINE, 16)
-    temp, flux = solved(jnp.stack([space, line]).astype(jnp.int32), sums, own, south, north, known)
-
-    def unpacked(value):
-        lead = value.shape[:-3]
-        n = len(lead)
-        value = value.reshape(lead + (16, 8, 4, 32))[..., 8:24]
-        order = tuple(range(n)) + tuple(n + d for d in (3, 1, 2, 0))
-        return value.transpose(order).reshape(lead + (16, 8, 64))
-
-    return unpacked(temp), unpacked(flux)
+    temp, flux = solved(jnp.stack([space, line]).astype(jnp.int32), sums, own, south, north, wide)
+    return temp.reshape(16, 8, 64), flux.reshape(3, 16, 8, 64)
 
 
 def solution(mesh):

time: 112 us -> 92 us (0.82)
  the two profiles are of different devices: /device:TPU:57 before, /device:TPU:96 now
where the time goes in v2:
time: 92 us; the launch traced here: 91.5 us
  Pallas kernels  28.1 us (31%)
  blocking collectives  28.1 us (31%)
  waiting for transfers between devices  18.6 us (20%)
  starting transfers between devices  10.3 us (11%)
  local copies, waits for them, and re-layouts  3.99 us (4%)
  other arithmetic  1.79 us (2%)
    all_to_all x1, blocking collectives, per_device(): got = lax.all_to_all(paired, ('space', 'zy'), 0, 0, tiled=True)  28.1 us
    pallas_call x1, Pallas kernels, moments(): pl.pallas_call(moments_kernel, grid=(SLAB,), in_specs=[pl.BlockSpec(memor...  18.7 us
    ppermute x4, waiting for transfers between devices, both_ways(): return (lax.ppermute(value, axis, ahead), lax.ppermute(value, axis, behind))  15.8 us
    ppermute x4, starting transfers between devices, both_ways(): return (lax.ppermute(value, axis, ahead), lax.ppermute(value, axis, behind))  10.2 us
    pallas_call x1, Pallas kernels, solved(): pl.pallas_call(solve_kernel, in_specs=[smem, smem, vmem] + [pl.BlockSpec(...  4.41 us
    unnamed x12, local copies, waits for them, and re-layouts  3.99 us
    pallas_call x1, Pallas kernels, gathered(): pl.pallas_call(gather_kernel, out_shape=[jax.ShapeDtypeStruct((6, 16, 8,...  2.87 us
    ppermute x1, waiting for transfers between devices, per_device(): received = lax.ppermute(send, 'core', [(0, 1), (1, 0)])  2.83 us
  transfers between devices with their start and end apart: 5, of which 5 were waited for; matrix products, arithmetic and copies ran while one was open for 0% of the time, Pallas kernels for 0%

profile of v2, /device:TPU:96, one launch (start us, length us, event | category | flops | bytes accessed | tf_op | source)
XLA Modules:
  0.0 91.5 jit_solution(15435167551216241485)
XLA Ops:
  0.6 0.1 pad_add_fusion.1.idx_ref
  0.7 0.7 convert_bitcast_fusion
  1.4 0.7 pad_maximum_fusion.par_ref
  2.1 0.0 copy-start.3
  2.1 0.7 copy-done.3
  2.7 18.7 %moments.1 = (f32[64,72,128]{2,1,0:T(8,128)S(1)}, bf16[64,72,128]{2,1,0:T(8,128)(2,1)S(1)}) custom-call(s32[2]{0:T(128)S(1)} %pad_add_fusion.1.idx_ref, f32[6]{0:T(128)S(1)} %copy-done.3, f32[4,48]{1,0:T(4,128)S(1)} %pad_maximum_fusion.par_ref, bf16[48,8,128,128]{3,2,1,0:T(8,128)(2,1)} %e_ref.1), custom_call_target="tpu_custom_call" | custom-call | flops 20000000000 | bytes 16000000 | tf_op jit(solution)/shard_map/moments/pallas_call | solution.py:261
  21.4 0.1 collective-permute-start
  21.5 2.8 %collective-permute-done = bf16[64,72,128]{2,1,0:T(8,128)(2,1)S(1)} collective-permute-done((bf16[64,72,128]{2,1,0:T(8,128)(2,1)S(1)}, bf16[64,72,128]{2,1,0:T(8,128)(2,1)S(1)}, u32[]{:S(2)}, u32[]{:S(2)}) %collective-permute-start) | collective-permute-done | bytes 1179680 | tf_op jit(solution)/shard_map/ppermute | solution.py:584
  24.3 0.3 add_convert_fusion
  24.6 28.1 %all_to_all.5.got_ref = bf16[64,72,128]{2,1,0:T(8,128)(2,1)} all-to-all(bf16[64,72,128]{2,1,0:T(8,128)(2,1)S(1)} %add_convert_fusion), channel_id=1, replica_groups=mesh['space'=8,'zy'=8,'core'=2] {'space','zy'}, dimensions={0} | all-to-all | bytes 2359296 | tf_op jit(solution)/shard_map/all_to_all | solution.py:586
  52.7 2.9 %gather.1 = (f32[6,16,8,128]{3,2,1,0:T(8,128)}, f32[2,128,128]{2,1,0:T(8,128)}, bf16[448,128]{1,0:T(8,128)(2,1)}, f32[8,128]{1,0:T(8,128)}) custom-call(bf16[64,72,128]{2,1,0:T(8,128)(2,1)} %all_to_all.5.got_ref, f32[128,64]{1,0:T(8,128)} %bitcast.14, f32[128,64]{1,0:T(8,128)} %bitcast.15, s32[128,64]{1,0:T(8,128)} %bitcast.16), custom_call_target="tpu_custom_call" | custom-call | tf_op jit(solution)/shard_map/gather/pallas_call | solution.py:351
  55.6 3.4 %collective-permute-start.2 = (bf16[448,128]{1,0:T(8,128)(2,1)}, bf16[448,128]{1,0:T(8,128)(2,1)S(1)}, u32[]{:S(2)}, u32[]{:S(2)}) collective-permute-start(bf16[448,128]{1,0:T(8,128)(2,1)} %get-tuple-element.17), channel_id=1, source_target_pairs={{16,0},{32,16},{48,32},{64,48},{80,64},{96,80},{112,96},{17,1},{33... | collective-permute-start | bytes 344072 | tf_op jit(solution)/shard_map/ppermute | solution.py:553
  59.1 2.4 %collective-permute-start.1 = (bf16[448,128]{1,0:T(8,128)(2,1)}, bf16[448,128]{1,0:T(8,128)(2,1)S(1)}, u32[]{:S(2)}, u32[]{:S(2)}) collective-permute-start(bf16[448,128]{1,0:T(8,128)(2,1)} %get-tuple-element.17), channel_id=1, source_target_pairs={{0,16},{16,32},{32,48},{48,64},{64,80},{80,96},{96,112},{1,17},{17... | collective-permute-start | bytes 344072 | tf_op jit(solution)/shard_map/ppermute | solution.py:553
  61.5 1.0 %collective-permute-done.2.east_ref = bf16[448,128]{1,0:T(8,128)(2,1)S(1)} collective-permute-done((bf16[448,128]{1,0:T(8,128)(2,1)}, bf16[448,128]{1,0:T(8,128)(2,1)S(1)}, u32[]{:S(2)}, u32[]{:S(2)}) %collective-permute-start.2) | collective-permute-done | bytes 114720 | tf_op jit(solution)/shard_map/ppermute | solution.py:553
  62.5 0.0 copy-start.4
  62.5 5.6 %collective-permute-done.1.west_ref = bf16[448,128]{1,0:T(8,128)(2,1)S(1)} collective-permute-done((bf16[448,128]{1,0:T(8,128)(2,1)}, bf16[448,128]{1,0:T(8,128)(2,1)S(1)}, u32[]{:S(2)}, u32[]{:S(2)}) %collective-permute-start.1) | collective-permute-done | bytes 114720 | tf_op jit(solution)/shard_map/ppermute | solution.py:553
  68.1 0.0 copy-start.5
  68.1 0.0 copy-done.4
  68.1 0.6 copy-done.5
  68.7 2.1 %widen.1 = (f32[7,16,8,128]{3,2,1,0:T(8,128)}, bf16[896,128]{1,0:T(8,128)(2,1)}) custom-call(f32[6,16,8,128]{3,2,1,0:T(8,128)} %get-tuple-element.15.own_ref, f32[2,128,128]{2,1,0:T(8,128)} %get-tuple-element.16.known_ref, bf16[448,128]{1,0:T(8,128)(2,1)} %copy-done.5, bf16[448,128]{1,0:T(8,128)(2,1)} %copy-done.4), custom_call_target="tpu_custom_call" | custom-call | tf_op jit(solution)/shard_map/widen/pallas_call | solution.py:380
  70.8 2.4 %collective-permute-start.4 = (bf16[896,128]{1,0:T(8,128)(2,1)}, bf16[896,128]{1,0:T(8,128)(2,1)S(1)}, u32[]{:S(2)}, u32[]{:S(2)}) collective-permute-start(bf16[896,128]{1,0:T(8,128)(2,1)} %get-tuple-element.18), channel_id=1, source_target_pairs={{1,0},{2,1},{3,2},{4,3},{5,4},{6,5},{7,6},{8,7},{9,8},{10,9},{11,1... | collective-permute-start | bytes 688136 | tf_op jit(solution)/shard_map/ppermute | solution.py:553
  73.3 1.9 %collective-permute-start.3 = (bf16[896,128]{1,0:T(8,128)(2,1)}, bf16[896,128]{1,0:T(8,128)(2,1)S(1)}, u32[]{:S(2)}, u32[]{:S(2)}) collective-permute-start(bf16[896,128]{1,0:T(8,128)(2,1)} %get-tuple-element.18), channel_id=1, source_target_pairs={{0,1},{1,2},{2,3},{3,4},{4,5},{5,6},{6,7},{7,8},{8,9},{9,10},{10,1... | collective-permute-start | bytes 688136 | tf_op jit(solution)/shard_map/ppermute | solution.py:553
  75.2 0.1 pad_add_fusion.idx_ref
  75.3 1.8 %collective-permute-done.4.north_hbm = bf16[896,128]{1,0:T(8,128)(2,1)S(1)} collective-permute-done((bf16[896,128]{1,0:T(8,128)(2,1)}, bf16[896,128]{1,0:T(8,128)(2,1)S(1)}, u32[]{:S(2)}, u32[]{:S(2)}) %collective-permute-start.4) | collective-permute-done | bytes 229408 | tf_op jit(solution)/shard_map/ppermute | solution.py:553
  77.1 7.3 %collective-permute-done.3.south_hbm = bf16[896,128]{1,0:T(8,128)(2,1)S(1)} collective-permute-done((bf16[896,128]{1,0:T(8,128)(2,1)}, bf16[896,128]{1,0:T(8,128)(2,1)S(1)}, u32[]{:S(2)}, u32[]{:S(2)}) %collective-permute-start.3) | collective-permute-done | bytes 229408 | tf_op jit(solution)/shard_map/ppermute | solution.py:553
  84.4 0.0 copy-start
  84.4 1.0 %copy-done = f32[6,16,8,128]{3,2,1,0:T(8,128)S(1)} copy-done((f32[6,16,8,128]{3,2,1,0:T(8,128)S(1)}, f32[6,16,8,128]{3,2,1,0:T(8,128)}, u32[]{:S(2)}) %copy-start) | copy-done | bytes 393240
  85.4 0.0 copy-start.1
  85.4 1.0 %copy-done.1 = f32[7,16,8,128]{3,2,1,0:T(8,128)S(1)} copy-done((f32[7,16,8,128]{3,2,1,0:T(8,128)S(1)}, f32[7,16,8,128]{3,2,1,0:T(8,128)}, u32[]{:S(2)}) %copy-start.1) | copy-done | bytes 458776
  86.4 0.0 copy-start.2
  86.5 0.7 copy-done.2
  87.1 4.4 %solve.1 = (f32[128,64]{1,0:T(8,128)}, f32[3,128,64]{2,1,0:T(8,128)}) custom-call(s32[2]{0:T(128)S(1)} %pad_add_fusion.idx_ref, f32[8,128]{1,0:T(8,128)S(1)} %copy-done.2, f32[6,16,8,128]{3,2,1,0:T(8,128)S(1)} %copy-done, bf16[896,128]{1,0:T(8,128)(2,1)S(1)} %collective-permute-done.3.south_hbm, bf16[896,128]{1,0:T(8,128)(2,1)S(1)} %collective-permute-done.4.north_hbm, ...), custom_call_target="tpu_custom_call" | custom-call | tf_op jit(solution)/shard_map/solve/pallas_call | solution.py:529
Async XLA Ops:
  2.1 0.7 copy-start.3
  21.4 2.9 %collective-permute-start = (bf16[64,72,128]{2,1,0:T(8,128)(2,1)S(1)}, bf16[64,72,128]{2,1,0:T(8,128)(2,1)S(1)}, u32[]{:S(2)}, u32[]{:S(2)}) collective-permute-start(bf16[64,72,128]{2,1,0:T(8,128)(2,1)S(1)} %get-tuple-element.13), channel_id=1, source_target_pairs={{0,1},{1,0},{2,3},{3,2},{4,5},{5,4},{6,7},{7,6},{8,9},{9,8},{10,11... | collective-permute-start | bytes 3538952 | tf_op jit(solution)/shard_map/ppermute | solution.py:584
  55.6 6.9 %collective-permute-start.2 = (bf16[448,128]{1,0:T(8,128)(2,1)}, bf16[448,128]{1,0:T(8,128)(2,1)S(1)}, u32[]{:S(2)}, u32[]{:S(2)}) collective-permute-start(bf16[448,128]{1,0:T(8,128)(2,1)} %get-tuple-element.17), channel_id=1, source_target_pairs={{16,0},{32,16},{48,32},{64,48},{80,64},{96,80},{112,96},{17,1},{33... | collective-permute-start | bytes 344072 | tf_op jit(solution)/shard_map/ppermute | solution.py:553
  59.1 9.0 %collective-permute-start.1 = (bf16[448,128]{1,0:T(8,128)(2,1)}, bf16[448,128]{1,0:T(8,128)(2,1)S(1)}, u32[]{:S(2)}, u32[]{:S(2)}) collective-permute-start(bf16[448,128]{1,0:T(8,128)(2,1)} %get-tuple-element.17), channel_id=1, source_target_pairs={{0,16},{16,32},{32,48},{48,64},{64,80},{80,96},{96,112},{1,17},{17... | collective-permute-start | bytes 344072 | tf_op jit(solution)/shard_map/ppermute | solution.py:553
  62.5 5.6 %copy-start.4 = (bf16[448,128]{1,0:T(8,128)(2,1)}, bf16[448,128]{1,0:T(8,128)(2,1)S(1)}, u32[]{:S(2)}) copy-start(bf16[448,128]{1,0:T(8,128)(2,1)S(1)} %collective-permute-done.2.east_ref) | copy-start | bytes 344068
  68.1 0.6 copy-start.5
  70.8 6.3 %collective-permute-start.4 = (bf16[896,128]{1,0:T(8,128)(2,1)}, bf16[896,128]{1,0:T(8,128)(2,1)S(1)}, u32[]{:S(2)}, u32[]{:S(2)}) collective-permute-start(bf16[896,128]{1,0:T(8,128)(2,1)} %get-tuple-element.18), channel_id=1, source_target_pairs={{1,0},{2,1},{3,2},{4,3},{5,4},{6,5},{7,6},{8,7},{9,8},{10,9},{11,1... | collective-permute-start | bytes 688136 | tf_op jit(solution)/shard_map/ppermute | solution.py:553
  73.3 11.2 %collective-permute-start.3 = (bf16[896,128]{1,0:T(8,128)(2,1)}, bf16[896,128]{1,0:T(8,128)(2,1)S(1)}, u32[]{:S(2)}, u32[]{:S(2)}) collective-permute-start(bf16[896,128]{1,0:T(8,128)(2,1)} %get-tuple-element.18), channel_id=1, source_target_pairs={{0,1},{1,2},{2,3},{3,4},{4,5},{5,6},{6,7},{7,8},{8,9},{9,10},{10,1... | collective-permute-start | bytes 688136 | tf_op jit(solution)/shard_map/ppermute | solution.py:553
  84.4 1.0 %copy-start = (f32[6,16,8,128]{3,2,1,0:T(8,128)S(1)}, f32[6,16,8,128]{3,2,1,0:T(8,128)}, u32[]{:S(2)}) copy-start(f32[6,16,8,128]{3,2,1,0:T(8,128)} %get-tuple-element.15.own_ref) | copy-start | bytes 1179652
  85.4 1.0 %copy-start.1 = (f32[7,16,8,128]{3,2,1,0:T(8,128)S(1)}, f32[7,16,8,128]{3,2,1,0:T(8,128)}, u32[]{:S(2)}) copy-start(f32[7,16,8,128]{3,2,1,0:T(8,128)} %get-tuple-element.19.wide_ref) | copy-start | bytes 1376260
  86.4 0.7 copy-start.2

commit v3 on v2

--- a/solution.py
+++ b/solution.py
@@ -42,14 +42,15 @@
     return lax.broadcasted_iota(jnp.int32, shape, len(shape) - 1)
 
 
-def mode_rows(table, prop_ref):
-    branch = table[0:1]
-    orient = table[1:2]
-    cap = table[2:3] / float(MODES)
-    rate = 1.0 / table[3:4]
+def mode_rows(table):
+    labels = table[0:1, :]
+    branch = sum(jnp.where(labels >= 16.0 * b, 1.0, 0.0) for b in range(1, 6))
+    orient = labels - 16.0 * branch
+    cap = table[1:2, :] / float(MODES)
+    rate = 1.0 / table[2:3, :]
     speed = jnp.zeros_like(branch)
     for b in range(6):
-        speed = speed + jnp.where(branch == float(b), prop_ref[b], 0.0)
+        speed = speed + jnp.where(branch == float(b), table[3:4, b : b + 1], 0.0)
     polar = jnp.where(orient >= 4.0, 1.0, 0.0) + jnp.where(orient >= 8.0, 1.0, 0.0)
     polar = polar + jnp.where(orient >= 12.0, 1.0, 0.0)
     turn = orient - 4.0 * polar
@@ -89,11 +90,12 @@
     )
 
 
-def build_tables(par_ref, prop_ref, par5, coef):
+def build_tables(par_ref, par5, coef):
     par5[...] = jnp.ones(par5.shape, F32)
-    for o in range(5):
-        par5[0:4, o * LOCAL : (o + 1) * LOCAL] = par_ref[...]
-    vx, vy, vz, rate, _ = mode_rows(par5[0:4, :], prop_ref)
+    for n in range(4):
+        for o in range(5):
+            par5[n : n + 1, o * LOCAL : (o + 1) * LOCAL] = par_ref[:, n * LOCAL : (n + 1) * LOCAL]
+    vx, vy, vz, rate, _ = mode_rows(par5)
     one, two = step_terms(vx, vy, vz, rate)
     weights = fields_on_rows(vx, vy, vz, rate)
     lane = lane_iota((1, DEPTH))
@@ -122,8 +124,8 @@
     coef[...] = jnp.concatenate(parts + [rest], axis=0).astype(BF16)
 
 
-def mode_sums(par_ref, prop_ref, core):
-    vx, vy, vz, rate, cap = mode_rows(par_ref[...], prop_ref)
+def mode_sums(par5, core):
+    vx, vy, vz, rate, cap = mode_rows(par5)
     one, _ = step_terms(vx, vy, vz, rate)
     weights = fields_on_rows(vx, vy, vz, rate)
     gain = STEP * rate * cap
@@ -133,17 +135,18 @@
             columns.append(weights * gain * jnp.where(v * sign > 0.0, value, 0.0))
     columns.append(weights * gain)
     columns.append(jnp.broadcast_to(cap * rate, weights.shape))
+    mine = lane_iota(weights.shape) < LOCAL
     lane = lane_iota((8, 128))
     sums = jnp.zeros((8, 128), F32)
     for n, column in enumerate(columns):
-        sums = jnp.where(lane == n, jnp.sum(column, axis=1, keepdims=True), sums)
+        sums = jnp.where(lane == n, jnp.sum(jnp.where(mine, column, 0.0), axis=1, keepdims=True), sums)
     row = lax.broadcasted_iota(jnp.int32, (8, 128), 0)
     sums = jnp.where((row // 4) == core, sums, 0.0)
     high = sums.astype(BF16).astype(F32)
     return high, pltpu.roll(sums - high, 48, 1)
 
 
-def moments_kernel(idx_ref, prop_ref, par_ref, e_ref, keep_ref, send_ref, par5, coef, spread, turned, acc, drift):
+def moments_kernel(idx_ref, par_ref, e_ref, keep_ref, send_ref, par5, coef, spread, turned, acc, drift):
     z = pl.program_id(0)
     space = idx_ref[0]
     core = idx_ref[1]
@@ -151,7 +154,7 @@
 
     @pl.when(z == 0)
     def _():
-        build_tables(par_ref, prop_ref, par5, coef)
+        build_tables(par_ref, par5, coef)
         turned[0 : 2 * LOCAL, :] = jnp.zeros((2 * LOCAL, 128), BF16)
         turned[(NX + 2) * LOCAL :, :] = jnp.zeros((2 * LOCAL + 16, 128), BF16)
 
@@ -234,7 +237,7 @@
         for zo in range(EXT):
             drift[zo * NX : zo * NX + NX, :] = divergence(zo)
         rows = (0, None, 5, 6, 7, 4)
-        extras = mode_sums(par_ref, prop_ref, core)
+        extras = mode_sums(par5, core)
 
         def strip(depth, i):
             f, zo = divmod(depth, EXT)
@@ -256,15 +259,14 @@
                     send_ref[8 * i + p, 8 * d : 8 * d + 8, :] = sent.astype(BF16)
 
 
-def moments(idx, prop, par, state):
+def moments(idx, table, state):
     whole = pl.BlockSpec((64, PIECE, 128), lambda z: (0, 0, 0))
     return pl.pallas_call(
         moments_kernel,
         grid=(SLAB,),
         in_specs=[
             pl.BlockSpec(memory_space=pltpu.SMEM),
-            pl.BlockSpec(memory_space=pltpu.SMEM),
-            pl.BlockSpec((4, LOCAL), lambda z: (0, 0)),
+            pl.BlockSpec((1, 4 * LOCAL), lambda z: (0, 0)),
             pl.BlockSpec((LOCAL, 1, NX, NY), lambda z: (0, z, 0, 0)),
         ],
         out_specs=[whole, whole],
@@ -280,13 +282,15 @@
         compiler_params=pltpu.CompilerParams(vmem_limit_bytes=48 << 20),
         cost_estimate=pl.CostEstimate(flops=20_000_000_000, bytes_accessed=16_000_000, transcendentals=0),
         name="moments",
-    )(idx, prop, par, state)
-
-
-def gather_kernel(got_ref, temp_ref, bulk_ref, label_ref, own_ref, known_ref, edge_ref, sums_ref, total):
+    )(idx, table, state)
+
+
+def gather_kernel(
+    got_ref, temp_ref, bulk_ref, label_ref, own_ref, known_ref, east_ref, west_ref, sums_ref, total
+):
     lane = lane_iota((8, 128))
     group = lane // 32
-    inner = (lane % 32 >= 8) & (lane % 32 < 24)
+    eighth = (lane % 32) // 8
     for s in range(8):
         for d in range(DEPTHS):
             value = got_ref[8 * s, 8 * d : 8 * d + 8, :].astype(F32)
@@ -341,9 +345,16 @@
                 return own_ref[n, zz]
             return known_ref[n - 5, 8 * zz : 8 * zz + 8, :]
 
-        for h in range(8):
-            packed = jnp.where(inner, cells(2 * h), pltpu.roll(cells(2 * h + 1), 16, 1))
-            edge_ref[(n * 8 + h) * 8 : (n * 8 + h) * 8 + 8, :] = packed.astype(BF16)
+        for h in range(4):
+            rows = slice((n * 4 + h) * 8, (n * 4 + h) * 8 + 8)
+            for ref, first in ((east_ref, 16), (west_ref, 8)):
+                packed = None
+                for k in range(4):
+                    turn = (8 * k - first) % 128
+                    value = cells(4 * h + k)
+                    value = pltpu.roll(value, turn, 1) if turn else value
+                    packed = value if k == 0 else jnp.where(eighth == k, value, packed)
+                ref[rows, :] = packed.astype(BF16)
 
 
 def gathered(got, temp, bulk, label):
@@ -353,7 +364,8 @@
         out_shape=[
             jax.ShapeDtypeStruct((6, 16, 8, 128), F32),
             jax.ShapeDtypeStruct((2, 128, 128), F32),
-            jax.ShapeDtypeStruct((7 * 64, 128), BF16),
+            jax.ShapeDtypeStruct((7 * 32, 128), BF16),
+            jax.ShapeDtypeStruct((7 * 32, 128), BF16),
             jax.ShapeDtypeStruct((8, 128), F32),
         ],
         scratch_shapes=[pltpu.VMEM((8 * DEPTHS, 8, 128), F32)],
@@ -361,42 +373,62 @@
     )(got, *flat)
 
 
-def widen_kernel(own_ref, known_ref, west_ref, east_ref, wide_ref, halo_ref):
+FULL = (1, 5, 6)
+HALVES = ((0, 2), (3, 4))
+HALO = (len(FULL) + len(HALVES)) * 128
+
+
+def widen_kernel(idx_ref, own_ref, known_ref, west_ref, east_ref, wide_ref, cross_ref, partner_ref):
     part = lane_iota((8, 128)) % 32
-    for n in range(7):
-        for zz in range(16):
-            at = (n * 8 + zz // 2) * 8
-            west = pltpu.roll(west_ref[at : at + 8, :].astype(F32), 96 if zz % 2 else 112, 1)
-            east = east_ref[at : at + 8, :].astype(F32)
-            if zz % 2 == 0:
-                east = pltpu.roll(east, 16, 1)
-            own = own_ref[n, zz] if n < 5 else known_ref[n - 5, 8 * zz : 8 * zz + 8, :]
-            value = jnp.where(part < 8, west, jnp.where(part < 24, own, east))
-            wide_ref[n, zz] = value
-            halo_ref[(n * 16 + zz) * 8 : (n * 16 + zz) * 8 + 8, :] = value.astype(BF16)
-
-
-def widened(own, known, west, east):
+    row = lax.broadcasted_iota(jnp.int32, (8, 128), 0)
+    core = idx_ref[1]
+
+    def cells(n, zz):
+        at = (n * 4 + zz // 4) * 8
+        k = zz % 4
+        west = west_ref[at : at + 8, :].astype(F32)
+        west = pltpu.roll(west, 128 - 8 * k, 1) if k else west
+        east = east_ref[at : at + 8, :].astype(F32)
+        east = pltpu.roll(east, 24 - 8 * k, 1) if k < 3 else east
+        own = own_ref[n, zz] if n < 5 else known_ref[n - 5, 8 * zz : 8 * zz + 8, :]
+        value = jnp.where(part < 8, west, jnp.where(part < 24, own, east))
+        wide_ref[n, zz] = value
+        return value
+
+    for zz in range(16):
+        wide_ref[7, zz] = own_ref[5, zz]
+        for u, n in enumerate(FULL):
+            value = cells(n, zz).astype(BF16)
+            at = (u * 16 + zz) * 8
+            cross_ref[at : at + 8, :] = value
+            partner_ref[at : at + 8, :] = value
+        for u, (n, m) in enumerate(HALVES):
+            value = cells(n, zz)
+            other = pltpu.roll(cells(m, zz), 4, 0)
+            southward = jnp.where(row < 4, value, other)
+            northward = jnp.where(row < 4, other, value)
+            at = ((len(FULL) + u) * 16 + zz) * 8
+            cross_ref[at : at + 8, :] = jnp.where(core == 0, southward, northward).astype(BF16)
+            partner_ref[at : at + 8, :] = jnp.where(core == 0, northward, southward).astype(BF16)
+
+
+def widened(idx, own, known, west, east):
+    vmem = pl.BlockSpec(memory_space=pltpu.VMEM)
     return pl.pallas_call(
         widen_kernel,
+        in_specs=[pl.BlockSpec(memory_space=pltpu.SMEM)] + [vmem] * 4,
         out_shape=[
-            jax.ShapeDtypeStruct((7, 16, 8, 128), F32),
-            jax.ShapeDtypeStruct((7 * 128, 128), BF16),
+            jax.ShapeDtypeStruct((8, 16, 8, 128), F32),
+            jax.ShapeDtypeStruct((HALO, 128), BF16),
+            jax.ShapeDtypeStruct((HALO, 128), BF16),
         ],
         name="widen",
-    )(own, known, west, east)
-
-
-def solve_kernel(
-    idx_ref, sums_ref, own_ref, south_hbm, north_hbm, wide_ref, temp_ref, flux_ref, halo, lines, sems
-):
-    copies = [
-        pltpu.make_async_copy(src, halo.at[n], sems.at[n]) for n, src in enumerate((south_hbm, north_hbm))
-    ]
-    for copy in copies:
-        copy.start()
-    for copy in copies:
-        copy.wait()
+    )(idx, own, known, west, east)
+
+
+def solve_kernel(idx_ref, sums_vmem, cross_ref, partner_ref, wide_ref, temp_ref, flux_ref, lines, sums_ref, sem):
+    copy = pltpu.make_async_copy(sums_vmem, sums_ref, sem)
+    copy.start()
     shape = (16, 24, 128)
     lane = lane_iota((1, 24, 128))
     x = lane % 32 + (idx_ref[0] * 16 - 8)
@@ -404,17 +436,25 @@
     inside = jnp.where((x >= 0) & (x < NX) & (y >= 0) & (y < NY), 1.0, 0.0)
     group = lane_iota((1, 24, 128)) // 32
 
-    def wide(own, f):
-        rows = slice(f * 128, f * 128 + 128)
-        south = halo[0, rows, :].astype(F32).reshape(16, 8, 128)
-        north = halo[1, rows, :].astype(F32).reshape(16, 8, 128)
-        return jnp.concatenate([south, own, north], axis=1)
+    def sent(ref, f):
+        if f in FULL:
+            u = FULL.index(f)
+            return ref[u * 128 : u * 128 + 128, :].astype(F32).reshape(16, 8, 128)
+        u, second = next((u, pair.index(f)) for u, pair in enumerate(HALVES) if f in pair)
+        at = (len(FULL) + u) * 128
+        value = ref[at : at + 128, :].astype(F32).reshape(16, 8, 128)
+        return pltpu.roll(value, 4, 1) if second else value
 
     def field(f):
-        return wide(wide_ref[f], f)
+        cross = sent(cross_ref, f)
+        partner = sent(partner_ref, f)
+        first = idx_ref[2] == 0
+        south = jnp.where(first, cross, partner)
+        north = jnp.where(first, partner, cross)
+        return jnp.concatenate([south, wide_ref[f], north], axis=1)
 
     def known(n):
-        return wide(wide_ref[5 + n], 5 + n)
+        return field(5 + n)
 
     def east(v):
         return pltpu.roll(v, 127, 2)
@@ -436,10 +476,6 @@
         edge = jnp.where(group > 0, pltpu.roll(v[15:16], 32, 2), 0.0)
         return jnp.concatenate([edge, v[:-1]], axis=0)
 
-    total_scalar = sums_ref[0, 8]
-    total = jnp.full((1, 24, 128), total_scalar, F32)
-    theta = total + 6.0
-    sigma = theta / 6.0
     kappa = known(1)
 
     def face(a, b):
@@ -453,6 +489,11 @@
     face_w = west(face_e)
     face_s = south(face_n)
     face_d = below(face_u)
+
+    copy.wait()
+    total = jnp.full((1, 24, 128), sums_ref[0, 8], F32)
+    theta = total + 6.0
+    sigma = theta / 6.0
 
     def operator(v):
         out = face_e * (east(v) - v) + face_w * (west(v) - v)
@@ -489,7 +530,7 @@
         return value
 
     flux = [second(k, field(k + 1)) * inside for k in (1, 2, 3)]
-    own = own_ref[5]
+    own = wide_ref[7]
     energy = second(0, jnp.concatenate([own, own, own], axis=1))
     rhs = -0.5 * (
         (east(flux[0]) - west(flux[0])) + (north(flux[1]) - south(flux[1])) + (above(flux[2]) - below(flux[2]))
@@ -523,34 +564,27 @@
         write(n + 1, flux[n], store_flux)
 
 
-def solved(idx, sums, own, south, north, wide):
+def solved(idx, sums, cross, partner, wide):
     vmem = pl.BlockSpec(memory_space=pltpu.VMEM)
-    smem = pl.BlockSpec(memory_space=pltpu.SMEM)
     return pl.pallas_call(
         solve_kernel,
-        in_specs=[smem, smem, vmem] + [pl.BlockSpec(memory_space=pl.ANY)] * 2 + [vmem],
+        in_specs=[pl.BlockSpec(memory_space=pltpu.SMEM)] + [vmem] * 4,
         out_specs=[vmem, vmem],
         out_shape=[
             jax.ShapeDtypeStruct((128, 64), F32),
             jax.ShapeDtypeStruct((3, 128, 64), F32),
         ],
         scratch_shapes=[
-            pltpu.VMEM((2, 7 * 128, 128), BF16),
             pltpu.VMEM((4, 16 * PACE, 128), F32),
-            pltpu.SemaphoreType.DMA((2,)),
+            pltpu.SMEM((8, 128), F32),
+            pltpu.SemaphoreType.DMA(()),
         ],
         compiler_params=pltpu.CompilerParams(vmem_limit_bytes=48 << 20),
         name="solve",
-    )(idx, sums, own, south, north, wide)
+    )(idx, sums, cross, partner, wide)
 
 
 LINE = ("zy", "core")
-
-
-def both_ways(value, axis, count):
-    ahead = [(i, i + 1) for i in range(count - 1)]
-    behind = [(i + 1, i) for i in range(count - 1)]
-    return lax.ppermute(value, axis, ahead), lax.ppermute(value, axis, behind)
 
 
 def per_device(
@@ -567,28 +601,32 @@
     space = lax.axis_index("space")
     core = lax.axis_index("core")
     line = lax.axis_index("zy") * 2 + core
-    table = jnp.stack(
+    idx = jnp.stack([space, core]).astype(jnp.int32)
+    labels = state_polarization_label * 16 + state_orientation_label
+    table = jnp.concatenate(
         [
-            state_polarization_label.astype(F32),
-            state_orientation_label.astype(F32),
+            labels.astype(F32),
             state_specific_warmth_scaled,
             scattering_lifetimes,
+            polarization_propagation_rate,
+            jnp.zeros((LOCAL - 6,), F32),
         ]
-    )
-    keep, send = moments(
-        jnp.stack([space, core]).astype(jnp.int32),
-        polarization_propagation_rate,
-        table,
-        excess_phonon_enthalpy,
-    )
+    ).reshape(1, 4 * LOCAL)
+    keep, send = moments(idx, table, excess_phonon_enthalpy)
     received = lax.ppermute(send, "core", [(0, 1), (1, 0)])
     paired = (keep + received.astype(F32)).astype(BF16)
     got = lax.all_to_all(paired, ("space", "zy"), 0, 0, tiled=True)
-    own, known, edge, sums = gathered(got, thermal_offset, thermal_conductance_bulk, substance_label)
-    west, east = both_ways(edge, "space", 8)
-    wide, halo = widened(own, known, west, east)
-    south, north = both_ways(halo, LINE, 16)
-    temp, flux = solved(jnp.stack([space, line]).astype(jnp.int32), sums, own, south, north, wide)
+    own, known, eastward, westward, sums = gathered(
+        got, thermal_offset, thermal_conductance_bulk, substance_label
+    )
+    west = lax.ppermute(eastward, "space", [(i, i + 1) for i in range(7)])
+    east = lax.ppermute(westward, "space", [(i + 1, i) for i in range(7)])
+    wide, cross, partner = widened(idx, own, known, west, east)
+    across = [(2 * p + 1, 2 * p + 2) for p in range(7)]
+    cross = lax.ppermute(cross, LINE, across + [(b, a) for a, b in across])
+    partner = lax.ppermute(partner, "core", [(0, 1), (1, 0)])
+    place = jnp.stack([space, line, core]).astype(jnp.int32)
+    temp, flux = solved(place, sums, cross, partner, wide)
     return temp.reshape(16, 8, 64), flux.reshape(3, 16, 8, 64)
 
 

time: 92 us -> 86.7 us (0.942)
  the two profiles are of different devices: /device:TPU:96 before, /device:TPU:70 now
where the time goes in v3:
time: 86.7 us; the launch traced here: 86.3 us
  Pallas kernels  28.3 us (33%)
  blocking collectives  27 us (31%)
  waiting for transfers between devices  17 us (20%)
  starting transfers between devices  9.15 us (11%)
  local copies, waits for them, and re-layouts  3.1 us (4%)
  other arithmetic  1.06 us (1%)
    all_to_all x1, blocking collectives, per_device(): got = lax.all_to_all(paired, ('space', 'zy'), 0, 0, tiled=True)  27 us
    pallas_call x1, Pallas kernels, moments(): pl.pallas_call(moments_kernel, grid=(SLAB,), in_specs=[pl.BlockSpec(memor...  18.8 us
    ppermute x1, waiting for transfers between devices, per_device(): cross = lax.ppermute(cross, LINE, across + [(b, a) for a, b in across])  7.72 us
    ppermute x1, waiting for transfers between devices, per_device(): east = lax.ppermute(westward, 'space', [(i + 1, i) for i in range(7)])  6.27 us
    ppermute x1, starting transfers between devices, per_device(): west = lax.ppermute(eastward, 'space', [(i, i + 1) for i in range(7)])  4.49 us
    pallas_call x1, Pallas kernels, solved(): pl.pallas_call(solve_kernel, in_specs=[pl.BlockSpec(memory_space=pltpu.SM...  4.33 us
    pallas_call x1, Pallas kernels, gathered(): pl.pallas_call(gather_kernel, out_shape=[jax.ShapeDtypeStruct((6, 16, 8,...  2.97 us
    ppermute x1, waiting for transfers between devices, per_device(): received = lax.ppermute(send, 'core', [(0, 1), (1, 0)])  2.83 us
  transfers between devices with their start and end apart: 5, of which 4 were waited for; matrix products, arithmetic and copies ran while one was open for 0% of the time, Pallas kernels for 0%

profile of v3, /device:TPU:70, one launch (start us, length us, event | category | flops | bytes accessed | tf_op | source)
XLA Modules:
  0.0 86.3 jit_solution(10500042411908296550)
XLA Ops:
  0.6 0.1 pad_add_fusion.1.idx_ref
  0.7 0.0 copy-start.2
  0.7 0.7 add_convert_fusion.1
  1.4 0.8 concatenate.3
  2.2 18.8 %moments.1 = (f32[64,72,128]{2,1,0:T(8,128)S(1)}, bf16[64,72,128]{2,1,0:T(8,128)(2,1)S(1)}) custom-call(s32[2]{0:T(128)S(1)} %pad_add_fusion.1.idx_ref, f32[1,192]{1,0:T(1,128)S(1)} %bitcast.9, bf16[48,8,128,128]{3,2,1,0:T(8,128)(2,1)} %e_ref.1), custom_call_target="tpu_custom_call" | custom-call | flops 20000000000 | bytes 16000000 | tf_op jit(solution)/shard_map/moments/pallas_call | solution.py:264
  21.0 0.0 copy-done.2
  21.0 0.1 collective-permute-start
  21.1 2.8 %collective-permute-done = bf16[64,72,128]{2,1,0:T(8,128)(2,1)S(1)} collective-permute-done((bf16[64,72,128]{2,1,0:T(8,128)(2,1)S(1)}, bf16[64,72,128]{2,1,0:T(8,128)(2,1)S(1)}, u32[]{:S(2)}, u32[]{:S(2)}) %collective-permute-start) | collective-permute-done | bytes 1179680 | tf_op jit(solution)/shard_map/ppermute | solution.py:616
  23.9 0.2 add_convert_fusion
  24.2 27.0 %all_to_all.5.got_ref = bf16[64,72,128]{2,1,0:T(8,128)(2,1)} all-to-all(bf16[64,72,128]{2,1,0:T(8,128)(2,1)S(1)} %add_convert_fusion), channel_id=1, replica_groups=mesh['space'=8,'zy'=8,'core'=2] {'space','zy'}, dimensions={0} | all-to-all | bytes 2359296 | tf_op jit(solution)/shard_map/all_to_all | solution.py:618
  51.2 3.0 %gather.1 = (f32[6,16,8,128]{3,2,1,0:T(8,128)}, f32[2,128,128]{2,1,0:T(8,128)}, bf16[224,128]{1,0:T(8,128)(2,1)}, bf16[224,128]{1,0:T(8,128)(2,1)}, f32[8,128]{1,0:T(8,128)}) custom-call(bf16[64,72,128]{2,1,0:T(8,128)(2,1)} %all_to_all.5.got_ref, f32[128,64]{1,0:T(8,128)} %bitcast.10, f32[128,64]{1,0:T(8,128)} %bitcast.11, s32[128,64]{1,0:T(8,128)} %bitcast.12), custom_call_target="tpu_custom_call" | custom-call | tf_op jit(solution)/shard_map/gather/pallas_call | solution.py:362
  54.2 4.5 %collective-permute-start.1 = (bf16[224,128]{1,0:T(8,128)(2,1)}, bf16[224,128]{1,0:T(8,128)(2,1)S(1)}, u32[]{:S(2)}, u32[]{:S(2)}) collective-permute-start(bf16[224,128]{1,0:T(8,128)(2,1)} %get-tuple-element.19), channel_id=1, source_target_pairs={{0,16},{16,32},{32,48},{48,64},{64,80},{80,96},{96,112},{1,17},{17... | collective-permute-start | bytes 172040 | tf_op jit(solution)/shard_map/ppermute | solution.py:622
  58.7 1.9 %collective-permute-start.2 = (bf16[224,128]{1,0:T(8,128)(2,1)}, bf16[224,128]{1,0:T(8,128)(2,1)S(1)}, u32[]{:S(2)}, u32[]{:S(2)}) collective-permute-start(bf16[224,128]{1,0:T(8,128)(2,1)} %get-tuple-element.20), channel_id=1, source_target_pairs={{16,0},{32,16},{48,32},{64,48},{80,64},{96,80},{112,96},{17,1},{33... | collective-permute-start | bytes 172040 | tf_op jit(solution)/shard_map/ppermute | solution.py:623
  60.6 0.2 collective-permute-done.1.west_ref
  60.8 0.0 copy-start.3
  60.8 6.3 %collective-permute-done.2.east_ref = bf16[224,128]{1,0:T(8,128)(2,1)S(1)} collective-permute-done((bf16[224,128]{1,0:T(8,128)(2,1)}, bf16[224,128]{1,0:T(8,128)(2,1)S(1)}, u32[]{:S(2)}, u32[]{:S(2)}) %collective-permute-start.2) | collective-permute-done | bytes 57376 | tf_op jit(solution)/shard_map/ppermute | solution.py:623
  67.1 0.0 copy-start.4
  67.1 0.0 copy-done.3
  67.1 0.6 copy-done.4
  67.7 2.1 %widen.1 = (f32[8,16,8,128]{3,2,1,0:T(8,128)}, bf16[640,128]{1,0:T(8,128)(2,1)}, bf16[640,128]{1,0:T(8,128)(2,1)}) custom-call(s32[2]{0:T(128)} %copy-done.2, f32[6,16,8,128]{3,2,1,0:T(8,128)} %get-tuple-element.17.own_ref, f32[2,128,128]{2,1,0:T(8,128)} %get-tuple-element.18.known_ref, bf16[224,128]{1,0:T(8,128)(2,1)} %copy-done.3, bf16[224,128]{1,0:T(8,128)(2,1)} %copy-done.4), custom_call_target="tpu_custom_call" | custom-call | tf_op jit(solution)/shard_map/widen/pallas_call | solution.py:417
  69.8 1.9 %collective-permute-start.3 = (bf16[640,128]{1,0:T(8,128)(2,1)}, bf16[640,128]{1,0:T(8,128)(2,1)S(1)}, u32[]{:S(2)}, u32[]{:S(2)}) collective-permute-start(bf16[640,128]{1,0:T(8,128)(2,1)} %get-tuple-element.21), channel_id=1, source_target_pairs={{1,2},{3,4},{5,6},{7,8},{9,10},{11,12},{13,14},{2,1},{4,3},{6,5},{... | collective-permute-start | bytes 491528 | tf_op jit(solution)/shard_map/ppermute | solution.py:626
  71.7 0.7 collective-permute-start.4
  72.5 0.1 pad_add_fusion.idx_ref
  72.6 7.7 %collective-permute-done.3.cross_ref = bf16[640,128]{1,0:T(8,128)(2,1)S(1)} collective-permute-done((bf16[640,128]{1,0:T(8,128)(2,1)}, bf16[640,128]{1,0:T(8,128)(2,1)S(1)}, u32[]{:S(2)}, u32[]{:S(2)}) %collective-permute-start.3) | collective-permute-done | bytes 163872 | tf_op jit(solution)/shard_map/ppermute | solution.py:626
  80.3 0.0 collective-permute-done.4.partner_ref
  80.3 0.0 copy-start
  80.3 1.0 %copy-done = f32[8,16,8,128]{3,2,1,0:T(8,128)S(1)} copy-done((f32[8,16,8,128]{3,2,1,0:T(8,128)S(1)}, f32[8,16,8,128]{3,2,1,0:T(8,128)}, u32[]{:S(2)}) %copy-start) | copy-done | bytes 524312
  81.3 0.0 copy-start.1
  81.3 0.7 copy-done.1
  82.0 4.3 %solve.1 = (f32[128,64]{1,0:T(8,128)}, f32[3,128,64]{2,1,0:T(8,128)}) custom-call(s32[3]{0:T(128)S(1)} %pad_add_fusion.idx_ref, f32[8,128]{1,0:T(8,128)S(1)} %copy-done.1, bf16[640,128]{1,0:T(8,128)(2,1)S(1)} %collective-permute-done.3.cross_ref, bf16[640,128]{1,0:T(8,128)(2,1)S(1)} %collective-permute-done.4.partner_ref, f32[8,16,8,128]{3,2,1,0:T(8,128)S(1)} %copy-done), custom_call_target="tpu_custom_call" | custom-call | tf_op jit(solution)/shard_map/solve/pallas_call | solution.py:569
  (1 shorter events, 0.0 us)
Async XLA Ops:
  0.7 20.3 %copy-start.2 = (s32[2]{0:T(128)}, s32[2]{0:T(128)S(1)}, u32[]{:S(2)}) copy-start(s32[2]{0:T(128)S(1)} %pad_add_fusion.1.idx_ref) | copy-start | bytes 28
  21.0 2.9 %collective-permute-start = (bf16[64,72,128]{2,1,0:T(8,128)(2,1)S(1)}, bf16[64,72,128]{2,1,0:T(8,128)(2,1)S(1)}, u32[]{:S(2)}, u32[]{:S(2)}) collective-permute-start(bf16[64,72,128]{2,1,0:T(8,128)(2,1)S(1)} %get-tuple-element.15), channel_id=1, source_target_pairs={{0,1},{1,0},{2,3},{3,2},{4,5},{5,4},{6,7},{7,6},{8,9},{9,8},{10,11... | collective-permute-start | bytes 3538952 | tf_op jit(solution)/shard_map/ppermute | solution.py:616
  54.2 6.6 %collective-permute-start.1 = (bf16[224,128]{1,0:T(8,128)(2,1)}, bf16[224,128]{1,0:T(8,128)(2,1)S(1)}, u32[]{:S(2)}, u32[]{:S(2)}) collective-permute-start(bf16[224,128]{1,0:T(8,128)(2,1)} %get-tuple-element.19), channel_id=1, source_target_pairs={{0,16},{16,32},{32,48},{48,64},{64,80},{80,96},{96,112},{1,17},{17... | collective-permute-start | bytes 172040 | tf_op jit(solution)/shard_map/ppermute | solution.py:622
  58.7 8.4 %collective-permute-start.2 = (bf16[224,128]{1,0:T(8,128)(2,1)}, bf16[224,128]{1,0:T(8,128)(2,1)S(1)}, u32[]{:S(2)}, u32[]{:S(2)}) collective-permute-start(bf16[224,128]{1,0:T(8,128)(2,1)} %get-tuple-element.20), channel_id=1, source_target_pairs={{16,0},{32,16},{48,32},{64,48},{80,64},{96,80},{112,96},{17,1},{33... | collective-permute-start | bytes 172040 | tf_op jit(solution)/shard_map/ppermute | solution.py:623
  60.8 6.3 %copy-start.3 = (bf16[224,128]{1,0:T(8,128)(2,1)}, bf16[224,128]{1,0:T(8,128)(2,1)S(1)}, u32[]{:S(2)}) copy-start(bf16[224,128]{1,0:T(8,128)(2,1)S(1)} %collective-permute-done.1.west_ref) | copy-start | bytes 172036
  67.1 0.6 copy-start.4
  69.8 10.4 %collective-permute-start.3 = (bf16[640,128]{1,0:T(8,128)(2,1)}, bf16[640,128]{1,0:T(8,128)(2,1)S(1)}, u32[]{:S(2)}, u32[]{:S(2)}) collective-permute-start(bf16[640,128]{1,0:T(8,128)(2,1)} %get-tuple-element.21), channel_id=1, source_target_pairs={{1,2},{3,4},{5,6},{7,8},{9,10},{11,12},{13,14},{2,1},{4,3},{6,5},{... | collective-permute-start | bytes 491528 | tf_op jit(solution)/shard_map/ppermute | solution.py:626
  71.7 8.5 %collective-permute-start.4 = (bf16[640,128]{1,0:T(8,128)(2,1)}, bf16[640,128]{1,0:T(8,128)(2,1)S(1)}, u32[]{:S(2)}, u32[]{:S(2)}) collective-permute-start(bf16[640,128]{1,0:T(8,128)(2,1)} %get-tuple-element.22), channel_id=1, source_target_pairs={{0,1},{1,0},{2,3},{3,2},{4,5},{5,4},{6,7},{7,6},{8,9},{9,8},{10,11... | collective-permute-start | bytes 491528 | tf_op jit(solution)/shard_map/ppermute | solution.py:627
  80.3 1.0 %copy-start = (f32[8,16,8,128]{3,2,1,0:T(8,128)S(1)}, f32[8,16,8,128]{3,2,1,0:T(8,128)}, u32[]{:S(2)}) copy-start(f32[8,16,8,128]{3,2,1,0:T(8,128)} %get-tuple-element.23.wide_ref) | copy-start | bytes 1572868
  81.3 0.7 copy-start.1

commit v4 on v3

--- a/solution.py
+++ b/solution.py
@@ -369,6 +369,7 @@
             jax.ShapeDtypeStruct((8, 128), F32),
         ],
         scratch_shapes=[pltpu.VMEM((8 * DEPTHS, 8, 128), F32)],
+        compiler_params=pltpu.CompilerParams(vmem_limit_bytes=16 << 20),
         name="gather",
     )(got, *flat)
 
@@ -422,6 +423,7 @@
             jax.ShapeDtypeStruct((HALO, 128), BF16),
             jax.ShapeDtypeStruct((HALO, 128), BF16),
         ],
+        compiler_params=pltpu.CompilerParams(vmem_limit_bytes=8 << 20),
         name="widen",
     )(idx, own, known, west, east)
 
@@ -579,7 +581,7 @@
             pltpu.SMEM((8, 128), F32),
             pltpu.SemaphoreType.DMA(()),
         ],
-        compiler_params=pltpu.CompilerParams(vmem_limit_bytes=48 << 20),
+        compiler_params=pltpu.CompilerParams(vmem_limit_bytes=16 << 20),
         name="solve",
     )(idx, sums, cross, partner, wide)
 

time: 86.7 us -> 80.4 us (0.927)
  Pallas kernels: 28.3 us -> 24.8 us
  local copies, waits for them, and re-layouts: 3.1 us -> 0.78 us
    unnamed x10 -> x6, local copies, waits for them, and re-layouts: 2.34 us -> 0.02 us
    pallas_call x1, Pallas kernels: 2.97 us -> 0.93 us  [gathered(): pl.pallas_call(gather_kernel, out_shape=[jax.ShapeDtypeStruct((6, 16, 8,...]
    pallas_call x1, Pallas kernels: 2.14 us -> 0.71 us  [widened(): pl.pallas_call(widen_kernel, in_specs=[pl.BlockSpec(memory_space=pltpu.SM...]
  transfers between devices with their start and end apart: 5 -> 5, of which waited for: 4 -> 3; matrix products, arithmetic and copies ran while one was open for 0% -> 0% of each run, Pallas kernels for 0% -> 0%
where the time goes in v4:
time: 80.4 us; the launch traced here: 80.1 us
  blocking collectives  27 us (34%)
  Pallas kernels  24.8 us (31%)
  waiting for transfers between devices  16.6 us (21%)
  starting transfers between devices  9.17 us (11%)
  other arithmetic  1.06 us (1%)
    all_to_all x1, blocking collectives, per_device(): got = lax.all_to_all(paired, ('space', 'zy'), 0, 0, tiled=True)  27 us
    pallas_call x1, Pallas kernels, moments(): pl.pallas_call(moments_kernel, grid=(SLAB,), in_specs=[pl.BlockSpec(memor...  18.8 us
    ppermute x1, waiting for transfers between devices, per_device(): cross = lax.ppermute(cross, LINE, across + [(b, a) for a, b in across])  7.51 us
    ppermute x1, waiting for transfers between devices, per_device(): east = lax.ppermute(westward, 'space', [(i + 1, i) for i in range(7)])  6.24 us
    ppermute x1, starting transfers between devices, per_device(): west = lax.ppermute(eastward, 'space', [(i, i + 1) for i in range(7)])  4.5 us
    pallas_call x1, Pallas kernels, solved(): pl.pallas_call(solve_kernel, in_specs=[pl.BlockSpec(memory_space=pltpu.SM...  4.3 us
    ppermute x1, waiting for transfers between devices, per_device(): received = lax.ppermute(send, 'core', [(0, 1), (1, 0)])  2.83 us
    ppermute x1, starting transfers between devices, per_device(): east = lax.ppermute(westward, 'space', [(i + 1, i) for i in range(7)])  1.92 us
  transfers between devices with their start and end apart: 5, of which 3 were waited for; matrix products, arithmetic and copies ran while one was open for 0% of the time, Pallas kernels for 0%

profile of v4, /device:TPU:70, one launch (start us, length us, event | category | flops | bytes accessed | tf_op | source)
XLA Modules:
  0.0 80.1 jit_solution(18354933981454437449)
XLA Ops:
  0.6 0.1 pad_add_fusion.1.idx_ref
  0.7 0.7 add_convert_fusion.1
  1.4 0.8 concatenate.3
  2.2 18.8 %moments.1 = (f32[64,72,128]{2,1,0:T(8,128)S(1)}, bf16[64,72,128]{2,1,0:T(8,128)(2,1)S(1)}) custom-call(s32[2]{0:T(128)S(1)} %pad_add_fusion.1.idx_ref, f32[1,192]{1,0:T(1,128)S(1)} %bitcast.12, bf16[48,8,128,128]{3,2,1,0:T(8,128)(2,1)} %e_ref.1), custom_call_target="tpu_custom_call" | custom-call | flops 20000000000 | bytes 16000000 | tf_op jit(solution)/shard_map/moments/pallas_call | solution.py:264
  21.0 0.1 collective-permute-start
  21.1 2.8 %collective-permute-done = bf16[64,72,128]{2,1,0:T(8,128)(2,1)S(1)} collective-permute-done((bf16[64,72,128]{2,1,0:T(8,128)(2,1)S(1)}, bf16[64,72,128]{2,1,0:T(8,128)(2,1)S(1)}, u32[]{:S(2)}, u32[]{:S(2)}) %collective-permute-start) | collective-permute-done | bytes 1179680 | tf_op jit(solution)/shard_map/ppermute | solution.py:618
  23.9 0.2 add_convert_fusion
  24.1 0.0 copy-start
  24.2 0.0 copy-start.1
  24.2 0.0 copy-start.2
  24.2 27.0 %all_to_all.5.got_ref = bf16[64,72,128]{2,1,0:T(8,128)(2,1)S(1)} all-to-all(bf16[64,72,128]{2,1,0:T(8,128)(2,1)S(1)} %add_convert_fusion), channel_id=1, replica_groups=mesh['space'=8,'zy'=8,'core'=2] {'space','zy'}, dimensions={0} | all-to-all | bytes 2359296 | tf_op jit(solution)/shard_map/all_to_all | solution.py:620
  51.2 0.0 copy-done
  51.2 0.0 copy-done.1
  51.2 0.0 copy-done.2
  51.2 0.9 %gather.1 = (f32[6,16,8,128]{3,2,1,0:T(8,128)S(1)}, f32[2,128,128]{2,1,0:T(8,128)S(1)}, bf16[224,128]{1,0:T(8,128)(2,1)S(1)}, bf16[224,128]{1,0:T(8,128)(2,1)S(1)}, f32[8,128]{1,0:T(8,128)S(1)}) custom-call(bf16[64,72,128]{2,1,0:T(8,128)(2,1)S(1)} %all_to_all.5.got_ref, f32[128,64]{1,0:T(8,128)S(1)} %bitcast.9, f32[128,64]{1,0:T(8,128)S(1)} %bitcast.10, ...), custom_call_target="tpu_custom_call" | custom-call | tf_op jit(solution)/shard_map/gather/pallas_call | solution.py:362
  52.2 4.5 %collective-permute-start.1 = (bf16[224,128]{1,0:T(8,128)(2,1)S(1)}, bf16[224,128]{1,0:T(8,128)(2,1)S(1)}, u32[]{:S(2)}, u32[]{:S(2)}) collective-permute-start(bf16[224,128]{1,0:T(8,128)(2,1)S(1)} %get-tuple-element.19), channel_id=1, source_target_pairs={{0,16},{16,32},{32,48},{48,64},{64,80},{80,96},{96,112},{1,17},{17... | collective-permute-start | bytes 172040 | tf_op jit(solution)/shard_map/ppermute | solution.py:624
  56.7 1.9 %collective-permute-start.2 = (bf16[224,128]{1,0:T(8,128)(2,1)S(1)}, bf16[224,128]{1,0:T(8,128)(2,1)S(1)}, u32[]{:S(2)}, u32[]{:S(2)}) collective-permute-start(bf16[224,128]{1,0:T(8,128)(2,1)S(1)} %get-tuple-element.20), channel_id=1, source_target_pairs={{16,0},{32,16},{48,32},{64,48},{80,64},{96,80},{112,96},{17,1},{33... | collective-permute-start | bytes 172040 | tf_op jit(solution)/shard_map/ppermute | solution.py:625
  58.6 0.0 collective-permute-done.1.west_ref
  58.6 6.2 %collective-permute-done.2.east_ref = bf16[224,128]{1,0:T(8,128)(2,1)S(1)} collective-permute-done((bf16[224,128]{1,0:T(8,128)(2,1)S(1)}, bf16[224,128]{1,0:T(8,128)(2,1)S(1)}, u32[]{:S(2)}, u32[]{:S(2)}) %collective-permute-start.2) | collective-permute-done | bytes 57376 | tf_op jit(solution)/shard_map/ppermute | solution.py:625
  64.9 0.7 widen.1
  65.6 1.9 %collective-permute-start.3 = (bf16[640,128]{1,0:T(8,128)(2,1)S(1)}, bf16[640,128]{1,0:T(8,128)(2,1)S(1)}, u32[]{:S(2)}, u32[]{:S(2)}) collective-permute-start(bf16[640,128]{1,0:T(8,128)(2,1)S(1)} %get-tuple-element.21), channel_id=1, source_target_pairs={{1,2},{3,4},{5,6},{7,8},{9,10},{11,12},{13,14},{2,1},{4,3},{6,5},{... | collective-permute-start | bytes 491528 | tf_op jit(solution)/shard_map/ppermute | solution.py:628
  67.5 0.7 collective-permute-start.4
  68.3 0.1 pad_add_fusion.idx_ref
  68.3 7.5 %collective-permute-done.3.cross_ref = bf16[640,128]{1,0:T(8,128)(2,1)S(1)} collective-permute-done((bf16[640,128]{1,0:T(8,128)(2,1)S(1)}, bf16[640,128]{1,0:T(8,128)(2,1)S(1)}, u32[]{:S(2)}, u32[]{:S(2)}) %collective-permute-start.3) | collective-permute-done | bytes 163872 | tf_op jit(solution)/shard_map/ppermute | solution.py:628
  75.8 0.0 collective-permute-done.4.partner_ref
  75.8 4.3 %solve.1 = (f32[128,64]{1,0:T(8,128)}, f32[3,128,64]{2,1,0:T(8,128)}) custom-call(s32[3]{0:T(128)S(1)} %pad_add_fusion.idx_ref, f32[8,128]{1,0:T(8,128)S(1)} %get-tuple-element.16.sums_vmem, bf16[640,128]{1,0:T(8,128)(2,1)S(1)} %collective-permute-done.3.cross_ref, bf16[640,128]{1,0:T(8,128)(2,1)S(1)} %collective-permute-done.4.partner_ref, ...), custom_call_target="tpu_custom_call" | custom-call | tf_op jit(solution)/shard_map/solve/pallas_call | solution.py:571
  (1 shorter events, 0.0 us)
Async XLA Ops:
  21.0 2.9 %collective-permute-start = (bf16[64,72,128]{2,1,0:T(8,128)(2,1)S(1)}, bf16[64,72,128]{2,1,0:T(8,128)(2,1)S(1)}, u32[]{:S(2)}, u32[]{:S(2)}) collective-permute-start(bf16[64,72,128]{2,1,0:T(8,128)(2,1)S(1)} %get-tuple-element.15), channel_id=1, source_target_pairs={{0,1},{1,0},{2,3},{3,2},{4,5},{5,4},{6,7},{7,6},{8,9},{9,8},{10,11... | collective-permute-start | bytes 3538952 | tf_op jit(solution)/shard_map/ppermute | solution.py:618
  24.1 27.1 %copy-start = (f32[16,8,64]{2,1,0:T(8,128)S(1)}, f32[16,8,64]{2,1,0:T(8,128)}, u32[]{:S(2)}) copy-start(f32[16,8,64]{2,1,0:T(8,128)} %param.10) | copy-start | bytes 98308
  24.2 27.1 %copy-start.1 = (f32[16,8,64]{2,1,0:T(8,128)S(1)}, f32[16,8,64]{2,1,0:T(8,128)}, u32[]{:S(2)}) copy-start(f32[16,8,64]{2,1,0:T(8,128)} %param.16) | copy-start | bytes 98308
  24.2 27.1 %copy-start.2 = (s32[16,8,64]{2,1,0:T(8,128)S(1)}, s32[16,8,64]{2,1,0:T(8,128)}, u32[]{:S(2)}) copy-start(s32[16,8,64]{2,1,0:T(8,128)} %param.17) | copy-start | bytes 98308
  52.2 6.4 %collective-permute-start.1 = (bf16[224,128]{1,0:T(8,128)(2,1)S(1)}, bf16[224,128]{1,0:T(8,128)(2,1)S(1)}, u32[]{:S(2)}, u32[]{:S(2)}) collective-permute-start(bf16[224,128]{1,0:T(8,128)(2,1)S(1)} %get-tuple-element.19), channel_id=1, source_target_pairs={{0,16},{16,32},{32,48},{48,64},{64,80},{80,96},{96,112},{1,17},{17... | collective-permute-start | bytes 172040 | tf_op jit(solution)/shard_map/ppermute | solution.py:624
  56.7 8.2 %collective-permute-start.2 = (bf16[224,128]{1,0:T(8,128)(2,1)S(1)}, bf16[224,128]{1,0:T(8,128)(2,1)S(1)}, u32[]{:S(2)}, u32[]{:S(2)}) collective-permute-start(bf16[224,128]{1,0:T(8,128)(2,1)S(1)} %get-tuple-element.20), channel_id=1, source_target_pairs={{16,0},{32,16},{48,32},{64,48},{80,64},{96,80},{112,96},{17,1},{33... | collective-permute-start | bytes 172040 | tf_op jit(solution)/shard_map/ppermute | solution.py:625
  65.6 10.3 %collective-permute-start.3 = (bf16[640,128]{1,0:T(8,128)(2,1)S(1)}, bf16[640,128]{1,0:T(8,128)(2,1)S(1)}, u32[]{:S(2)}, u32[]{:S(2)}) collective-permute-start(bf16[640,128]{1,0:T(8,128)(2,1)S(1)} %get-tuple-element.21), channel_id=1, source_target_pairs={{1,2},{3,4},{5,6},{7,8},{9,10},{11,12},{13,14},{2,1},{4,3},{6,5},{... | collective-permute-start | bytes 491528 | tf_op jit(solution)/shard_map/ppermute | solution.py:628
  67.5 8.3 %collective-permute-start.4 = (bf16[640,128]{1,0:T(8,128)(2,1)S(1)}, bf16[640,128]{1,0:T(8,128)(2,1)S(1)}, u32[]{:S(2)}, u32[]{:S(2)}) collective-permute-start(bf16[640,128]{1,0:T(8,128)(2,1)S(1)} %get-tuple-element.22), channel_id=1, source_target_pairs={{0,1},{1,0},{2,3},{3,2},{4,5},{5,4},{6,7},{7,6},{8,9},{9,8},{10,11... | collective-permute-start | bytes 491528 | tf_op jit(solution)/shard_map/ppermute | solution.py:629
